TPU v7x, 32 devices: a whole 2x2x4 slice. The times are simulated.
32 devices in a mesh: dp: 4 (over z), tp: 8 (over y, x, core).
Axes of the slice: x: 2, y: 2, z: 4, core: 2. Of those that a mesh axis runs over, the one named last changes fastest.
Arguments:
- hidden: bfloat16 [4, 2048, 3072], P('dp', 'tp'), parts along dimension 0
- norm_attn: float32 [2, 3072], replicated
- w_q: bfloat16 [2, 3072, 24, 128], P(None, None, 'tp')
- w_kv: bfloat16 [2, 3072, 2, 8, 128], replicated
- w_o: bfloat16 [2, 24, 128, 3072], P(None, 'tp')
- norm_mlp: float32 [2, 3072], replicated
- w_gate: bfloat16 [2, 3072, 8192], P(None, None, 'tp')
- w_up: bfloat16 [2, 3072, 8192], P(None, None, 'tp')
- w_down: bfloat16 [2, 8192, 3072], P(None, 'tp')
Outputs:
- output: bfloat16 [4, 2048, 3072], P('dp', 'tp'), parts along dimension 0
There are 4 independent parts. A program takes and returns all parts, laid end to end along the dimension named above; an argument that names none is the same for every part.
All inputs are finite; a program needn't handle non-finite values.
Results may differ from a plain program's by a relative error of at most 0.0112868.
Values are sent between devices in bfloat16 or wider.
A program may use at most 1 GiB of HBM per device.

v0:
```python
import math
import jax
import jax.numpy as jnp
from jax import lax
from jax.sharding import PartitionSpec as P

EPS = 1e-5
ROPE_BASE = 10000.0


def rms_norm(resid, gain):
    mean_sq = jnp.mean(resid * resid, axis=-1, keepdims=True)
    return (resid * lax.rsqrt(mean_sq + EPS) * gain).astype(jnp.bfloat16)


def rope_tables(positions, head_dim):
    half_dim = head_dim // 2
    inv_freq = jnp.power(ROPE_BASE, -2.0 * jnp.arange(half_dim, dtype=jnp.float32) / head_dim)
    angles = positions.astype(jnp.float32)[:, None] * inv_freq[None, :]
    return jnp.cos(angles), jnp.sin(angles)


def apply_rope(proj, cos_t, sin_t):
    half_dim = proj.shape[-1] // 2
    first_half = proj[..., :half_dim]
    second_half = proj[..., half_dim:]
    cos_b = cos_t[None, :, None, :]
    sin_b = sin_t[None, :, None, :]
    return jnp.concatenate([first_half * cos_b - second_half * sin_b, second_half * cos_b + first_half * sin_b], axis=-1)


def solution(mesh):
    n_tp = mesh.shape['tp']
    tok_spec = P('dp', 'tp', None)
    in_specs = (tok_spec, P(), P(None, None, 'tp', None), P(), P(None, 'tp', None, None), P(), P(None, None, 'tp'), P(None, None, 'tp'), P(None, 'tp', None))

    def gather_rows(normed):
        return lax.all_gather(normed, 'tp', axis=1, tiled=True)

    def reduce_rows(partial):
        batch_loc, seq_len, width = partial.shape
        blocks = partial.astype(jnp.bfloat16).reshape(batch_loc, n_tp, seq_len // n_tp, width)
        received = lax.all_to_all(blocks, 'tp', 1, 1)
        return jnp.sum(received, axis=1, dtype=jnp.float32)

    def body(hidden, norm_attn, w_q, w_kv, w_o, norm_mlp, w_gate, w_up, w_down):
        n_layers = w_q.shape[0]
        heads_loc = w_q.shape[2]
        head_dim = w_q.shape[3]
        n_kv = w_kv.shape[3]
        kv_loc = max(1, n_kv // n_tp)
        group_loc = heads_loc // kv_loc
        batch_loc, rows_loc, _ = hidden.shape
        seq_len = rows_loc * n_tp
        kv_start = (lax.axis_index('tp') * n_kv) // n_tp
        positions = jnp.arange(seq_len)
        cos_t, sin_t = rope_tables(positions, head_dim)
        causal_mask = positions[:, None] >= positions[None, :]
        inv_sqrt = 1.0 / math.sqrt(head_dim)
        resid = hidden.astype(jnp.float32)
        for layer_idx in range(n_layers):
            gathered = gather_rows(rms_norm(resid, norm_attn[layer_idx]))
            kv_weight = lax.dynamic_slice_in_dim(w_kv[layer_idx], kv_start, kv_loc, axis=2)
            q_proj = jnp.einsum('bsd,dhe->bshe', gathered, w_q[layer_idx], preferred_element_type=jnp.float32)
            kv_proj = jnp.einsum('bsd,dcke->bscke', gathered, kv_weight, preferred_element_type=jnp.float32)
            queries = apply_rope(q_proj, cos_t, sin_t).astype(jnp.bfloat16).reshape(batch_loc, seq_len, kv_loc, group_loc, head_dim)
            keys = apply_rope(kv_proj[:, :, 0], cos_t, sin_t).astype(jnp.bfloat16)
            values = kv_proj[:, :, 1].astype(jnp.bfloat16)
            scores = jnp.einsum('bqkgd,bskd->bkgqs', queries, keys, preferred_element_type=jnp.float32) * inv_sqrt
            scores = jnp.where(causal_mask, scores, -jnp.inf)
            attn_probs = jax.nn.softmax(scores, axis=-1).astype(jnp.bfloat16)
            context = jnp.einsum('bkgqs,bskd->bqkgd', attn_probs, values, preferred_element_type=jnp.float32).astype(jnp.bfloat16)
            context = context.reshape(batch_loc, seq_len, heads_loc, head_dim)
            partial = jnp.einsum('bqhd,hdf->bqf', context, w_o[layer_idx], preferred_element_type=jnp.float32)
            resid = resid + reduce_rows(partial)
            gathered = gather_rows(rms_norm(resid, norm_mlp[layer_idx]))
            gate_proj = jnp.einsum('bsd,df->bsf', gathered, w_gate[layer_idx], preferred_element_type=jnp.float32)
            up_proj = jnp.einsum('bsd,df->bsf', gathered, w_up[layer_idx], preferred_element_type=jnp.float32)
            activated = (jax.nn.silu(gate_proj) * up_proj).astype(jnp.bfloat16)
            partial = jnp.einsum('bsf,fd->bsd', activated, w_down[layer_idx], preferred_element_type=jnp.float32)
            resid = resid + reduce_rows(partial)
        return resid.astype(jnp.bfloat16)

    return jax.shard_map(body, mesh=mesh, in_specs=in_specs, out_specs=tok_spec, check_vma=False)
```

profile of v0, /device:TPU:0, one launch (start us, length us, event | category | flops | bytes accessed | tf_op | source)
XLA Modules:
  0.0 1220.2 jit_solution(15873084648012938057)
XLA Ops:
  6.5 1.8 fusion.44
  9.8 3.0 fusion.46
  12.9 4.1 fusion.121
  17.0 2.5 copy.48
  19.5 10.5 fusion.120
  30.0 7.4 constant_dynamic-slice_fusion
  37.4 6.2 copy.22
  43.6 1.9 multiply_cosine_fusion
  45.5 4.1 iota_compare_fusion
  49.6 38.0 %all-gather.5.cloned.1.call-done = bf16[1,2048,3072]{2,1,0:T(8,128)(2,1)} async-done(((bf16[1,256,3072]{2,1,0:T(8,128)(2,1)}), bf16[1,2048,3072]{2,1,0:T(8,128)(2,1)}) %all-gather.5.cloned.1.call-update) | async-done | bytes 12582928 | tf_op jit(solution)/shard_map/all_gather | solution.py:38
  87.6 6.6 fusion.22
  94.4 2.8 fusion.109
  97.3 5.1 fusion.20
  104.6 18.3 %fusion.2 = (f32[3,2048]{1,0:T(4,128)S(1)}, f32[2048,2048,3]{1,0,2:T(8,128)}) fusion(pred[2048,2048]{0,1:T(8,128)(4,1)S(1)} %copy-done.4, bf16[2048,3,64]{0,2,1:T(8,128)(2,1)S(1)} %get-tuple-element.14, bf16[2048,3,64]{0,2,1:T(8,128)(2,1)S(1)} %get-tuple-element.13, bf16[2048,64]{0,1:T(8,128)(2,1)S(1)} %get-tuple-element.18, ...), kind=kOutput, calls=%fused_computation.8 | convolution fusion | flops 3263162368 | bytes 56647680 | tf_op jit(solution)/shard_map/bqkgd,bskd->bkgqs/dot_general | solution.py:69
  122.9 21.8 %fusion = f32[3,2048]{1,0:T(4,128)S(1)} fusion(f32[2048,2048,3]{1,0,2:T(8,128)} %get-tuple-element.26, f32[3,2048]{1,0:T(4,128)S(1)} %get-tuple-element.25, pred[2048,2048]{0,1:T(8,128)(4,1)} %iota_compare_fusion), kind=kLoop, calls=%fused_computation.6 | loop fusion | flops 50325504 | bytes 54575104 | tf_op jit(solution)/shard_map/reduce_sum | solution.py:71
  144.7 30.4 %bitcast_convert_fusion.1 = bf16[2048,3072]{1,0:T(8,128)(2,1)} fusion(f32[3,2048]{1,0:T(4,128)S(1)} %fusion, f32[3,2048]{1,0:T(4,128)S(1)} %get-tuple-element.25, f32[2048,2048,3]{1,0,2:T(8,128)} %get-tuple-element.26, pred[2048,2048]{0,1:T(8,128)(4,1)} %iota_compare_fusion, bf16[2,3,128,3072]{3,2,1,0:T(8,128)(2,1)} %param.13, ...), kind=kOutput, calls=%fused_computation.13 | convolution fusion | flops 8123056128 | bytes 70057984 | tf_op jit(solution)/shard_map/bqhd,hdf->bqf/dot_general | solution.py:74
  175.1 5.5 all-to-all-start
  181.3 138.3 %all-to-all-done = bf16[1,8,256,3072]{3,2,0,1:T(8,128)(2,1)} async-done(((bf16[1,8,256,3072]{3,2,0,1:T(8,128)(2,1)}), bf16[1,8,256,3072]{3,2,0,1:T(8,128)(2,1)}, u32[]{:S(2)}, u32[]{:S(2)}) %all-to-all-start) | async-done | bytes 12582944 | tf_op jit(solution)/shard_map/all_to_all | solution.py:43
  319.6 7.4 convert_reduce_fusion.3
  327.0 2.0 multiply_reduce_fusion.2
  329.1 1.7 multiply_convert_fusion.4
  330.9 71.0 %all-gather.7.cloned.1.call-done = bf16[1,2048,3072]{2,1,0:T(8,128)(2,1)} async-done(((bf16[1,256,3072]{2,1,0:T(8,128)(2,1)}), bf16[1,2048,3072]{2,1,0:T(8,128)(2,1)}) %all-gather.7.cloned.1.call-update) | async-done | bytes 12582928 | tf_op jit(solution)/shard_map/all_gather | solution.py:38
  401.9 18.3 %fusion.16 = f32[2048,1024]{1,0:T(8,128)S(1)} fusion(bf16[1,2048,3072]{2,1,0:T(8,128)(2,1)} %all-gather.7.cloned.1.call-done, bf16[2,3072,1024]{2,1,0:T(8,128)(2,1)} %param.16), kind=kOutput, calls=%fused_computation.29 | convolution fusion | flops 12884901888 | bytes 27262976 | tf_op jit(solution)/shard_map/bsd,df->bsf/dot_general | solution.py:78
  420.2 19.8 %multiply_convert_fusion.1 = bf16[2048,1024]{1,0:T(8,128)(2,1)} fusion(f32[2048,1024]{1,0:T(8,128)S(1)} %fusion.16, bf16[2,3072,1024]{2,1,0:T(8,128)(2,1)} %param.15, bf16[1,2048,3072]{2,1,0:T(8,128)(2,1)} %all-gather.7.cloned.1.call-done), kind=kOutput, calls=%fused_computation.40 | convolution fusion | flops 12897484800 | bytes 31457280 | tf_op jit(solution)/shard_map/bsd,df->bsf/dot_general | solution.py:77
  440.0 16.7 %convolution_convert_fusion.1 = bf16[2048,3072]{1,0:T(8,128)(2,1)S(1)} fusion(bf16[2048,1024]{1,0:T(8,128)(2,1)} %multiply_convert_fusion.1, bf16[2,1024,3072]{2,1,0:T(8,128)(2,1)} %param.17), kind=kOutput, calls=%fused_computation.38 | convolution fusion | flops 12891193344 | bytes 23068672 | tf_op jit(solution)/shard_map/bsf,fd->bsd/dot_general | solution.py:80
  456.7 142.5 %all_to_all.20 = bf16[1,8,256,3072]{3,2,0,1:T(8,128)(2,1)} all-to-all(bf16[1,8,256,3072]{3,2,0,1:T(8,128)(2,1)S(1)} %bitcast.242), channel_id=1, replica_groups=mesh['dp'=4,'tp'=8] {'tp'}, dimensions={1} | all-to-all | bytes 25165824 | tf_op jit(solution)/shard_map/all_to_all | solution.py:43
  599.2 9.1 convert_reduce_fusion.2
  608.2 3.0 multiply_reduce_fusion.1
  614.6 4.3 copy.49
  618.9 6.2 copy.30
  625.0 60.6 %all-gather.9.cloned.1.call-done = bf16[1,2048,3072]{2,1,0:T(8,128)(2,1)} async-done(((bf16[1,256,3072]{2,1,0:T(8,128)(2,1)}), bf16[1,2048,3072]{2,1,0:T(8,128)(2,1)}) %all-gather.9.cloned.1.call-update) | async-done | bytes 12582928 | tf_op jit(solution)/shard_map/all_gather | solution.py:38
  685.6 8.9 fusion.12
  696.0 3.5 fusion.14
  699.6 2.3 fusion.107
  701.9 18.4 %fusion.3 = (f32[3,2048]{1,0:T(4,128)S(1)}, f32[2048,2048,3]{1,0,2:T(8,128)}) fusion(pred[2048,2048]{0,1:T(8,128)(4,1)S(1)} %copy-done.5, bf16[2048,3,64]{0,2,1:T(8,128)(2,1)S(1)} %get-tuple-element.12, bf16[2048,3,64]{0,2,1:T(8,128)(2,1)S(1)} %get-tuple-element.11, bf16[2048,64]{0,1:T(8,128)(2,1)S(1)} %get-tuple-element.16, ...), kind=kOutput, calls=%fused_computation.9 | convolution fusion | flops 3263162368 | bytes 56647680 | tf_op jit(solution)/shard_map/bqkgd,bskd->bkgqs/dot_general | solution.py:69
  720.2 21.7 %fusion.1 = f32[3,2048]{1,0:T(4,128)S(1)} fusion(f32[2048,2048,3]{1,0,2:T(8,128)} %get-tuple-element.28, f32[3,2048]{1,0:T(4,128)S(1)} %get-tuple-element.27, pred[2048,2048]{0,1:T(8,128)(4,1)} %iota_compare_fusion), kind=kLoop, calls=%fused_computation.7 | loop fusion | flops 50325504 | bytes 54575104 | tf_op jit(solution)/shard_map/reduce_sum | solution.py:71
  741.9 30.6 %bitcast_convert_fusion = bf16[2048,3072]{1,0:T(8,128)(2,1)} fusion(f32[3,2048]{1,0:T(4,128)S(1)} %fusion.1, f32[3,2048]{1,0:T(4,128)S(1)} %get-tuple-element.27, f32[2048,2048,3]{1,0,2:T(8,128)} %get-tuple-element.28, pred[2048,2048]{0,1:T(8,128)(4,1)} %iota_compare_fusion, bf16[2,3,128,3072]{3,2,1,0:T(8,128)(2,1)} %param.13, ...), kind=kOutput, calls=%fused_computation.10 | convolution fusion | flops 8123056128 | bytes 70057984 | tf_op jit(solution)/shard_map/bqhd,hdf->bqf/dot_general | solution.py:74
  772.5 145.4 %all_to_all.21 = bf16[1,8,256,3072]{3,2,0,1:T(8,128)(2,1)} all-to-all(bf16[1,8,256,3072]{3,2,0,1:T(8,128)(2,1)} %bitcast.241), channel_id=1, replica_groups=mesh['dp'=4,'tp'=8] {'tp'}, dimensions={1} | all-to-all | bytes 25165824 | tf_op jit(solution)/shard_map/all_to_all | solution.py:43
  917.9 9.2 convert_reduce_fusion.1
  927.1 2.4 multiply_reduce_fusion
  930.0 1.9 multiply_convert_fusion.2
  931.9 71.1 %all-gather.11.cloned.1.call-done = bf16[1,2048,3072]{2,1,0:T(8,128)(2,1)} async-done(((bf16[1,256,3072]{2,1,0:T(8,128)(2,1)}), bf16[1,2048,3072]{2,1,0:T(8,128)(2,1)}) %all-gather.11.cloned.1.call-update) | async-done | bytes 12582928 | tf_op jit(solution)/shard_map/all_gather | solution.py:38
  1003.0 17.9 %fusion.8 = f32[2048,1024]{1,0:T(8,128)S(1)} fusion(bf16[1,2048,3072]{2,1,0:T(8,128)(2,1)} %all-gather.11.cloned.1.call-done, bf16[2,3072,1024]{2,1,0:T(8,128)(2,1)} %param.16), kind=kOutput, calls=%fused_computation.21 | convolution fusion | flops 12884901888 | bytes 27262976 | tf_op jit(solution)/shard_map/bsd,df->bsf/dot_general | solution.py:78
  1020.9 20.0 %multiply_convert_fusion = bf16[2048,1024]{1,0:T(8,128)(2,1)} fusion(f32[2048,1024]{1,0:T(8,128)S(1)} %fusion.8, bf16[2,3072,1024]{2,1,0:T(8,128)(2,1)} %param.15, bf16[1,2048,3072]{2,1,0:T(8,128)(2,1)} %all-gather.11.cloned.1.call-done), kind=kOutput, calls=%fused_computation.39 | convolution fusion | flops 12897484800 | bytes 31457280 | tf_op jit(solution)/shard_map/bsd,df->bsf/dot_general | solution.py:77
  1040.9 16.5 %convolution_convert_fusion = bf16[2048,3072]{1,0:T(8,128)(2,1)S(1)} fusion(bf16[2048,1024]{1,0:T(8,128)(2,1)} %multiply_convert_fusion, bf16[2,1024,3072]{2,1,0:T(8,128)(2,1)} %param.17), kind=kOutput, calls=%fused_computation.37 | convolution fusion | flops 12891193344 | bytes 23068672 | tf_op jit(solution)/shard_map/bsf,fd->bsd/dot_general | solution.py:80
  1057.4 142.5 %all_to_all.22 = bf16[1,8,256,3072]{3,2,0,1:T(8,128)(2,1)} all-to-all(bf16[1,8,256,3072]{3,2,0,1:T(8,128)(2,1)S(1)} %bitcast.243), channel_id=1, replica_groups=mesh['dp'=4,'tp'=8] {'tp'}, dimensions={1} | all-to-all | bytes 25165824 | tf_op jit(solution)/shard_map/all_to_all | solution.py:43
  1199.8 9.1 convert_reduce_fusion
  1208.9 4.6 fusion.47
  (71 shorter events, 9.9 us)
Async XLA Ops:
  6.5 81.1 %all-gather.5.cloned.1.call-start = ((), (), s32[]{:S(2)}) async-start(), calls=%async_computation.4 | async-start | bytes 14155776 | tf_op jit(solution)/shard_map/all_gather | solution.py:38
  43.5 44.1 %copy-start.13 = (bf16[1,3072,2,1,128]{1,4,2,3,0:T(8,128)(2,1)S(1)}, bf16[1,3072,2,1,128]{1,4,2,3,0:T(8,128)(2,1)}, u32[]{:S(2)}) copy-start(bf16[1,3072,2,1,128]{1,4,2,3,0:T(8,128)(2,1)} %copy.22) | copy-start | bytes 4718596
  43.6 50.8 %copy-start.21 = (f32[64]{0:T(128)}, f32[64]{0:T(128)S(1)}, u32[]{:S(2)}) copy-start(f32[64]{0:T(128)S(1)} %multiply_power_fusion) | copy-start | bytes 772
  43.6 50.8 %copy-start.16 = (f32[2048]{0:T(1024)}, f32[2048]{0:T(1024)S(1)}, u32[]{:S(2)}) copy-start(f32[2048]{0:T(1024)S(1)} %iota_convert_fusion) | copy-start | bytes 24580
  45.5 56.9 %copy-start.7 = (f32[2048,64]{0,1:T(8,128)}, f32[2048,64]{0,1:T(8,128)S(1)}, u32[]{:S(2)}) copy-start(f32[2048,64]{0,1:T(8,128)S(1)} %get-tuple-element.23) | copy-start | bytes 1572868
  45.5 56.9 %copy-start.9 = (f32[2048,64]{0,1:T(8,128)}, f32[2048,64]{0,1:T(8,128)S(1)}, u32[]{:S(2)}) copy-start(f32[2048,64]{0,1:T(8,128)S(1)} %get-tuple-element.24) | copy-start | bytes 1572868
  87.6 9.5 copy-start.11
  87.6 9.7 copy-start.23
  94.2 2.9 copy-start.14
  102.4 2.2 copy-start.4
  122.9 21.8 %copy-start.15 = (f32[2048,256]{0,1:S(1)}, f32[2048,256]{0,1}, u32[]{:S(2)}) copy-start(f32[2048,256]{0,1} %copy-done.14) | copy-start | bytes 6291460
  175.1 5.6 copy-start.20
  175.1 144.5 %all-to-all-start = ((bf16[1,8,256,3072]{3,2,0,1:T(8,128)(2,1)}), bf16[1,8,256,3072]{3,2,0,1:T(8,128)(2,1)}, u32[]{:S(2)}, u32[]{:S(2)}) async-start(bf16[1,8,256,3072]{3,2,0,1:T(8,128)(2,1)} %bitcast.240), calls=%async_computation | async-start | bytes 25165824 | tf_op jit(solution)/shard_map/all_to_all | solution.py:43
  180.6 221.3 %all-gather.7.cloned.1.call-start = ((), (), s32[]{:S(2)}) async-start(), calls=%async_computation.5 | async-start | bytes 14155776 | tf_op jit(solution)/shard_map/all_gather | solution.py:38
  327.0 2.0 copy-start.3
  330.8 354.8 %all-gather.9.cloned.1.call-start = ((), (), s32[]{:S(2)}) async-start(), calls=%async_computation.6 | async-start | bytes 14155776 | tf_op jit(solution)/shard_map/all_gather | solution.py:38
  608.2 4.7 copy-start.19
  611.2 1.7 copy-start
  612.9 6.0 copy-start.6
  614.5 388.5 %all-gather.11.cloned.1.call-start = ((), (), s32[]{:S(2)}) async-start(), calls=%async_computation.7 | async-start | bytes 14155776 | tf_op jit(solution)/shard_map/all_gather | solution.py:38
  685.6 8.9 copy-start.8
  685.6 9.0 copy-start.10
  685.6 9.5 copy-start.24
  694.5 1.5 copy-start.12
  696.0 3.5 copy-start.17
  696.0 3.6 copy-start.22
  696.0 5.9 copy-start.5
  917.9 9.2 copy-start.1
  927.1 2.8 copy-start.2
  927.1 2.8 copy-start.18
Sparse Core Ops, SparseCore 0:
  13.0 74.5 all-gather.4
  330.9 70.9 all-gather.6
  614.6 70.9 all-gather.8
  932.0 70.9 all-gather.10
where the time goes:
time: 1230 us; the launch traced here: 1220 us
  blocking collectives  430 us (35%)
  waiting for transfers between devices  379 us (31%)
  matrix products  231 us (19%)
  other arithmetic  112 us (9%)
  local copies, waits for them, and re-layouts  48.1 us (4%)
  between operations  13.7 us (1%)
    all_to_all x3, blocking collectives, reduce_rows(): received = lax.all_to_all(blocks, 'tp', 1, 1)  430 us
    all_gather x4, waiting for transfers between devices, gather_rows(): return lax.all_gather(normed, 'tp', axis=1, tiled=True)  241 us
    all_to_all x1, waiting for transfers between devices, reduce_rows(): received = lax.all_to_all(blocks, 'tp', 1, 1)  138 us
    dot_general x2, matrix products, body(): jnp.einsum('bqhd,hdf->bqf', context, w_o[layer_idx], preferred_element_ty...  61 us
    reduce_sum x2, other arithmetic, body(): attn_probs = jax.nn.softmax(scores, axis=-1).astype(jnp.bfloat16)  43.5 us
    dot_general x2, matrix products, body(): jnp.einsum('bsd,df->bsf', gathered, w_gate[layer_idx], preferred_element_...  39.8 us
    dot_general x2, matrix products, body(): jnp.einsum('bqkgd,bskd->bkgqs', queries, keys, preferred_element_type=jnp...  36.7 us
    dot_general x2, matrix products, body(): jnp.einsum('bsd,df->bsf', gathered, w_up[layer_idx], preferred_element_ty...  36.2 us
  transfers between devices with their start and end apart: 5, of which 5 were waited for; matrix products, arithmetic and copies ran while one was open for 4% of the time, Pallas kernels for 0%

commit v1 on v0

v1 whole, which is shorter than its diff:
```python
import functools
import math
import jax
import jax.numpy as jnp
from jax import lax
from jax.experimental import pallas as pl
from jax.experimental.pallas import tpu as pltpu
from jax.sharding import PartitionSpec as P

EPS = 1e-5
ROPE_BASE = 10000.0
MESH = pl.DeviceIdType.MESH
VMEM_LIMIT = 67043328
F32 = jnp.float32
BF16 = jnp.bfloat16
N_COPIES = 20


def dot(a, b):
    return jnp.dot(a, b, preferred_element_type=F32)


def places():
    me = lax.axis_index('tp')
    core = lax.rem(me, 2)
    x = lax.rem(lax.div(me, 2), 2)
    y = lax.div(me, 4)
    dx = 2 - 4 * x
    dy = 4 - 8 * y
    return me, me + 1 - 2 * core, dx, dy


def greet(pa, xn, yn):
    barrier = pltpu.get_barrier_semaphore()
    for dev in (pa, xn, yn):
        pl.semaphore_signal(barrier, inc=1, device_id={'tp': dev}, device_id_type=MESH)
    pl.semaphore_wait(barrier, 3)


def make_copies(G, PR, RX, RY, RD, S, ss, rs, pa, xn, yn):
    half = G.shape[1] // 2
    lo, hi = pl.ds(0, half), pl.ds(half, half)
    table = {
        'd1': (G.at[0], G.at[1], pa),
        'xh0': (G.at[0, lo], G.at[3, lo], xn),
        'yh1': (G.at[0, hi], G.at[3, hi], yn),
        'xf': (G.at[3, hi], G.at[5, hi], xn),
        'yf': (G.at[3, lo], G.at[5, lo], yn),
        'xh1': (G.at[0, hi], G.at[7, lo], xn),
        'yh0': (G.at[0, lo], G.at[7, hi], yn),
        'd2': (G.at[3], G.at[2], pa),
        'd4': (G.at[5], G.at[4], pa),
        'd6': (G.at[7], G.at[6], pa),
        'p1': (G.at[1], PR.at[0], pa),
        'p2': (G.at[2], PR.at[1], pa),
        'p4': (G.at[4], PR.at[2], pa),
        'p6': (G.at[6], PR.at[3], pa),
        'X0': (S.at[0, lo], RX.at[lo], xn),
        'Y1': (S.at[0, hi], RY.at[hi], yn),
        'D0': (S.at[1, lo], RD.at[hi], xn),
        'D1': (S.at[1, hi], RD.at[lo], yn),
        'X1': (S.at[2, lo], RX.at[hi], xn),
        'Y0': (S.at[2, hi], RY.at[lo], yn),
    }
    copies = {}
    for i, (name, (src, dst, dev)) in enumerate(table.items()):
        copies[name] = pltpu.make_async_remote_copy(
            src_ref=src, dst_ref=dst, send_sem=ss.at[i], recv_sem=rs.at[i],
            device_id={'tp': dev}, device_id_type=MESH)
    return copies


def start(copies, *names):
    for name in names:
        copies[name].start()


def arrived(copies, *names):
    for name in names:
        copies[name].wait_recv()


def norm_rows(r_ref, g_ref, G):
    rows = r_ref.shape[0]
    step = 32

    @pl.loop(0, rows // step)
    def _(i):
        at = pl.ds(pl.multiple_of(i * step, step), step)
        x = r_ref[at, :].astype(F32)
        mean_sq = jnp.mean(x * x, axis=-1, keepdims=True)
        G[0, at, :] = (x * lax.rsqrt(mean_sq + EPS) * g_ref[...]).astype(BF16)


def finish(copies, r_ref, acc0, PR, RX, RY, o_ref):
    arrived(copies, 'p1', 'X0', 'X1', 'Y0', 'Y1')
    rows = r_ref.shape[0]
    step = 32

    @pl.loop(0, rows // step)
    def _(i):
        at = pl.ds(pl.multiple_of(i * step, step), step)
        total = acc0[at, :] + PR[0, at, :].astype(F32)
        total += RX[at, :].astype(F32) + RY[at, :].astype(F32)
        o_ref[at, :] = (r_ref[at, :].astype(F32) + total).astype(o_ref.dtype)

    for copy in copies.values():
        copy.wait_send()


def project(a_ref, w_ref, width, emit):
    @pl.loop(0, w_ref.shape[1] // width)
    def _(n):
        cols = pl.ds(pl.multiple_of(n * width, width), width)
        emit(cols, dot(a_ref[...], w_ref[:, cols]))


def merge_last(copies, acc7, RD, S):
    arrived(copies, 'D0', 'D1')
    rows = acc7.shape[0]
    step = 32

    @pl.loop(0, rows // step)
    def _(i):
        at = pl.ds(pl.multiple_of(i * step, step), step)
        S[2, at, :] = (acc7[at, :] + RD[at, :].astype(F32)).astype(BF16)

    start(copies, 'X1', 'Y0')


def emitters(G, PR, S, acc0, acc7):
    def to_partner(j):
        def emit(cols, part):
            G[j, :, cols] = part.astype(BF16)
        return emit

    def chip_sum(i, slot):
        def emit(cols, part):
            S[slot, :, cols] = (part + PR[i, :, cols].astype(F32)).astype(BF16)
        return emit

    def own(cols, part):
        acc0[:, cols] = part

    def last(cols, part):
        acc7[:, cols] = part + PR[3, :, cols].astype(F32)

    return to_partner, chip_sum, own, last


def mlp_kernel(layer, r_ref, g_ref, wg_h, wu_h, wd_h, o_ref,
               wg, wu, wd, G, PR, RX, RY, RD, S, acc0, acc7, u, ss, rs, ls):
    me, pa, dx, dy = places()
    xn, yn = me + dx, me + dy
    loads = [pltpu.make_async_copy(h.at[layer], v, ls.at[i])
             for i, (h, v) in enumerate(((wg_h, wg), (wu_h, wu), (wd_h, wd)))]
    for load in loads:
        load.start()
    norm_rows(r_ref, g_ref, G)
    greet(pa, xn, yn)
    copies = make_copies(G, PR, RX, RY, RD, S, ss, rs, pa, xn, yn)
    to_partner, chip_sum, own, last = emitters(G, PR, S, acc0, acc7)
    start(copies, 'xh0', 'yh1', 'd1')

    def hidden(j):
        width = 256

        @pl.loop(0, wg.shape[1] // width)
        def _(n):
            cols = pl.ds(pl.multiple_of(n * width, width), width)
            gate = dot(G[j], wg[:, cols])
            up = dot(G[j], wu[:, cols])
            u[:, cols] = (jax.nn.silu(gate) * up).astype(BF16)

    def tile(j, emit):
        hidden(j)
        project(u, wd, 512, emit)

    for load in loads:
        load.wait()
    tile(0, own)
    arrived(copies, 'd1')
    tile(1, to_partner(1))
    start(copies, 'p1')
    arrived(copies, 'xh0', 'yh1')
    start(copies, 'xf', 'yf', 'd2', 'xh1', 'yh0')
    arrived(copies, 'd2')
    tile(2, to_partner(2))
    start(copies, 'p2')
    arrived(copies, 'p2')
    tile(3, chip_sum(1, 0))
    start(copies, 'X0', 'Y1')
    arrived(copies, 'xf', 'yf')
    start(copies, 'd4')
    arrived(copies, 'd4')
    tile(4, to_partner(4))
    start(copies, 'p4')
    arrived(copies, 'p4')
    tile(5, chip_sum(2, 1))
    start(copies, 'D0', 'D1')
    arrived(copies, 'xh1', 'yh0')
    start(copies, 'd6')
    arrived(copies, 'd6')
    tile(6, to_partner(6))
    start(copies, 'p6')
    arrived(copies, 'p6')
    tile(7, last)
    merge_last(copies, acc7, RD, S)
    finish(copies, r_ref, acc0, PR, RX, RY, o_ref)


def attn_kernel(layer, head_dim, r_ref, g_ref, cos_ref, sin_ref, wqkv_h, wo_h, o_ref,
                wqkv, wo, G, PR, RX, RY, RD, S, acc0, acc7, q_s, k_s, v_s, sc, l_s, ctx_acc, c_s, ss, rs, ls):
    me, pa, dx, dy = places()
    xn, yn = me + dx, me + dy
    loads = [pltpu.make_async_copy(h.at[layer], v, ls.at[i])
             for i, (h, v) in enumerate(((wqkv_h, wqkv), (wo_h, wo)))]
    for load in loads:
        load.start()
    norm_rows(r_ref, g_ref, G)
    greet(pa, xn, yn)
    copies = make_copies(G, PR, RX, RY, RD, S, ss, rs, pa, xn, yn)
    to_partner, chip_sum, own, last = emitters(G, PR, S, acc0, acc7)
    start(copies, 'xh0', 'yh1', 'd1')

    rows = r_ref.shape[0]
    half = rows // 2
    hd = head_dim
    group = wo.shape[0] // hd
    chunk = sc.shape[2]

    def halves(j):
        dev = me if j in (0, 3, 5, 7) else pa
        if j in (0, 1):
            first, second = dev, dev
        elif j in (4, 5):
            first = second = dev + dx + dy
        else:
            first, second = dev + dx, dev + dy
        if j in (6, 7):
            return first * rows + half, second * rows
        return first * rows, second * rows + half

    def qkv(j):
        for hh, pos in enumerate(halves(j)):
            pos = pl.multiple_of(pos, half)
            at = pl.ds(pos, half)
            proj = dot(G[j, hh * half:(hh + 1) * half, :], wqkv[...])
            cos_b = cos_ref[at, :]
            sin_b = sin_ref[at, :]

            def rope(n):
                part = proj[:, n * hd:(n + 1) * hd]
                return (part * cos_b + pltpu.roll(part, hd // 2, 1) * sin_b).astype(BF16)

            slot = lax.div(pos, half)
            for h in range(group):
                q_s[slot, h * half:(h + 1) * half, :] = rope(h)
            k_s[at, :] = rope(group)
            v_s[at, :] = proj[:, (group + 1) * hd:].astype(BF16)

    scale = math.log2(math.e) / math.sqrt(hd)

    def scores(q, start_key):
        keys = k_s[pl.ds(start_key, chunk), :]
        return lax.dot_general(q, keys, (((1,), (1,)), ((), ())), preferred_element_type=F32)

    def fold(s, op):
        out = s[:, :hd]
        for n in range(1, chunk // hd):
            out = op(out, s[:, n * hd:(n + 1) * hd])
        return out

    def attend(pos, out_row):
        q = q_s[lax.div(pos, half)]
        n_full = lax.div(pos, chunk)
        edge = pl.multiple_of(n_full * chunk, chunk)
        s = scores(q, edge)
        shape = (half, chunk)
        row = lax.broadcasted_iota(jnp.int32, shape, 0) + (pos - edge)
        keep = lax.broadcasted_iota(jnp.int32, shape, 1) <= row
        keep = jnp.concatenate([keep] * group, axis=0)
        s = jnp.where(keep, s, -jnp.inf)
        sc[n_full] = s
        l_s[...] = fold(s, jnp.maximum)

        @pl.loop(0, n_full)
        def _(c):
            s = scores(q, pl.multiple_of(c * chunk, chunk))
            sc[c] = s
            l_s[...] = jnp.maximum(l_s[...], fold(s, jnp.maximum))

        top = jnp.max(l_s[...], axis=1, keepdims=True)
        l_s[...] = jnp.zeros_like(l_s)
        ctx_acc[...] = jnp.zeros_like(ctx_acc)

        @pl.loop(0, n_full + 1)
        def _(c):
            p = jnp.exp2((sc[c] - top) * scale)
            l_s[...] += fold(p, jnp.add)
            ctx_acc[...] += dot(p.astype(BF16), v_s[pl.ds(pl.multiple_of(c * chunk, chunk), chunk), :])

        out = (ctx_acc[...] / jnp.sum(l_s[...], axis=1, keepdims=True)).astype(BF16)
        for h in range(group):
            c_s[pl.ds(out_row, half), h * hd:(h + 1) * hd] = out[h * half:(h + 1) * half, :]

    def tile(j, emit):
        first, second = halves(j)

        @pl.loop(0, 2)
        def _(hh):
            attend(pl.multiple_of(first + hh * (second - first), half), pl.multiple_of(hh * half, half))

        project(c_s, wo, 512, emit)

    loads[0].wait()
    qkv(0)
    arrived(copies, 'd1')
    qkv(1)
    arrived(copies, 'xh0', 'yh1')
    start(copies, 'xf', 'yf', 'd2', 'xh1', 'yh0')
    qkv(3)
    arrived(copies, 'd2')
    qkv(2)
    arrived(copies, 'xf', 'yf')
    start(copies, 'd4')
    qkv(5)
    arrived(copies, 'd4')
    qkv(4)
    arrived(copies, 'xh1', 'yh0')
    start(copies, 'd6')
    qkv(7)
    arrived(copies, 'd6')
    qkv(6)
    loads[1].wait()

    tile(4, to_partner(4))
    start(copies, 'p4')
    arrived(copies, 'p4')
    tile(5, chip_sum(2, 1))
    start(copies, 'D0', 'D1')
    tile(2, to_partner(2))
    start(copies, 'p2')
    arrived(copies, 'p2')
    tile(3, chip_sum(1, 0))
    start(copies, 'X0', 'Y1')
    tile(6, to_partner(6))
    start(copies, 'p6')
    arrived(copies, 'p6')
    tile(7, last)
    merge_last(copies, acc7, RD, S)
    tile(1, to_partner(1))
    start(copies, 'p1')
    tile(0, own)
    finish(copies, r_ref, acc0, PR, RX, RY, o_ref)


def comm_scratch(rows, width):
    return [
        pltpu.VMEM((8, rows, width), BF16),
        pltpu.VMEM((4, rows, width), BF16),
        pltpu.VMEM((rows, width), BF16),
        pltpu.VMEM((rows, width), BF16),
        pltpu.VMEM((rows, width), BF16),
        pltpu.VMEM((3, rows, width), BF16),
        pltpu.VMEM((rows, width), F32),
        pltpu.VMEM((rows, width), F32),
    ]


def semaphores(n_loads):
    return [pltpu.SemaphoreType.DMA((N_COPIES,)), pltpu.SemaphoreType.DMA((N_COPIES,)),
            pltpu.SemaphoreType.DMA((n_loads,))]


def call(kernel, collective, out_dtype, rows, width, n_vmem, n_any, scratch, name):
    vmem = pl.BlockSpec(memory_space=pltpu.VMEM)
    return pl.pallas_call(
        kernel,
        out_shape=jax.ShapeDtypeStruct((rows, width), out_dtype),
        in_specs=[vmem] * n_vmem + [pl.BlockSpec(memory_space=pl.ANY)] * n_any,
        out_specs=vmem,
        scratch_shapes=scratch,
        compiler_params=pltpu.CompilerParams(
            collective_id=collective, has_side_effects=True, vmem_limit_bytes=VMEM_LIMIT),
        name=name,
    )


def rope_tables(seq_len, head_dim):
    half_dim = head_dim // 2
    inv_freq = jnp.power(ROPE_BASE, -2.0 * jnp.arange(half_dim, dtype=F32) / head_dim)
    angles = jnp.arange(seq_len).astype(F32)[:, None] * inv_freq[None, :]
    cos_t, sin_t = jnp.cos(angles), jnp.sin(angles)
    return jnp.concatenate([cos_t, cos_t], axis=1), jnp.concatenate([-sin_t, sin_t], axis=1)


def solution(mesh):
    n_tp = mesh.shape['tp']
    tok_spec = P('dp', 'tp', None)
    in_specs = (tok_spec, P(), P(None, None, 'tp', None), P(), P(None, 'tp', None, None), P(), P(None, None, 'tp'), P(None, None, 'tp'), P(None, 'tp', None))

    def body(hidden, norm_attn, w_q, w_kv, w_o, norm_mlp, w_gate, w_up, w_down):
        n_layers, width, heads_loc, hd = w_q.shape
        rows = hidden.shape[1]
        seq_len = rows * n_tp
        half = rows // 2
        ff = w_gate.shape[2]
        chunk = 256
        head = lax.axis_index('tp')
        kv = lax.dynamic_slice_in_dim(w_kv, head, 1, axis=3).reshape(n_layers, width, 2 * hd)
        wqkv = jnp.concatenate([w_q.reshape(n_layers, width, heads_loc * hd), kv], axis=2)
        wo = w_o.reshape(n_layers, heads_loc * hd, width)
        cos_t, sin_t = rope_tables(seq_len, hd)
        attn_scratch = [
            pltpu.VMEM(wqkv.shape[1:], BF16), pltpu.VMEM(wo.shape[1:], BF16), *comm_scratch(rows, width),
            pltpu.VMEM((seq_len // half, heads_loc * half, hd), BF16),
            pltpu.VMEM((seq_len, hd), BF16), pltpu.VMEM((seq_len, hd), BF16),
            pltpu.VMEM((seq_len // chunk, heads_loc * half, chunk), F32),
            pltpu.VMEM((heads_loc * half, hd), F32), pltpu.VMEM((heads_loc * half, hd), F32),
            pltpu.VMEM((rows, heads_loc * hd), BF16), *semaphores(2)]
        mlp_scratch = [
            pltpu.VMEM((width, ff), BF16), pltpu.VMEM((width, ff), BF16), pltpu.VMEM((ff, width), BF16),
            *comm_scratch(rows, width), pltpu.VMEM((rows, ff), BF16), *semaphores(3)]
        resid = hidden[0]
        for layer in range(n_layers):
            out_dtype = BF16 if layer == n_layers - 1 else F32
            resid = call(functools.partial(attn_kernel, layer, hd), 2 * layer, F32, rows, width, 4, 2, attn_scratch, f'attn{layer}')(
                resid, norm_attn[layer][None, :], cos_t, sin_t, wqkv, wo)
            resid = call(functools.partial(mlp_kernel, layer), 2 * layer + 1, out_dtype, rows, width, 2, 3, mlp_scratch, f'mlp{layer}')(
                resid, norm_mlp[layer][None, :], w_gate, w_up, w_down)
        return resid[None]

    return jax.shard_map(body, mesh=mesh, in_specs=in_specs, out_specs=tok_spec, check_vma=False)
```

time: 1230 us -> 569 us (0.46)
  Pallas kernels: 0 us -> 505 us
  blocking collectives: 430 us -> 0 us
  waiting for transfers between devices: 379 us -> 0 us
  matrix products: 231 us -> 0 us
  other arithmetic: 112 us -> 11.9 us
  between operations: 13.7 us -> 0.49 us
    pallas_call x0 -> x4, Pallas kernels: none -> 505 us  [the longest x2 275 us: body(): call(functools.partial(attn_kernel, layer, hd), 2 * layer, F32, rows, wid...]
    all_to_all x3 -> x0, blocking collectives: 430 us -> none  [reduce_rows(): received = lax.all_to_all(blocks, 'tp', 1, 1)]
    all_gather x4 -> x0, waiting for transfers between devices: 241 us -> none  [gather_rows(): return lax.all_gather(normed, 'tp', axis=1, tiled=True)]
    dot_general x10 -> x0, matrix products: 207 us -> none  [the longest x2 61 us: body(): jnp.einsum('bqhd,hdf->bqf', context, w_o[layer_idx], preferred_element_ty...]
    all_to_all x1 -> x0, waiting for transfers between devices: 138 us -> none  [reduce_rows(): received = lax.all_to_all(blocks, 'tp', 1, 1)]
    reduce_sum x10 -> x0, other arithmetic: 87.5 us -> none  [the longest x2 43.5 us: body(): attn_probs = jax.nn.softmax(scores, axis=-1).astype(jnp.bfloat16)]
    unnamed x4 -> x0, matrix products: 24.1 us -> none
    slice x4 -> x2, local copies, waits for them, and re-layouts: 16.7 us -> 2.08 us  [the longest x1 1.45 us: body(): norm_mlp[layer][None, :]]
  transfers between devices with their start and end apart: 5 -> 0, of which waited for: 5 -> 0; matrix products, arithmetic and copies ran while one was open for 4% -> 0% of each run, Pallas kernels for 0% -> 0%
where the time goes in v1:
time: 569 us; the launch traced here: 563 us
  Pallas kernels  505 us (89%)
  local copies, waits for them, and re-layouts  45.6 us (8%)
  other arithmetic  11.9 us (2%)
    pallas_call x2, Pallas kernels, body(): call(functools.partial(attn_kernel, layer, hd), 2 * layer, F32, rows, wid...  275 us
    pallas_call x2, Pallas kernels, body(): call(functools.partial(mlp_kernel, layer), 2 * layer + 1, out_dtype, rows...  230 us
    unnamed x7, local copies, waits for them, and re-layouts  21.5 us
    dynamic_slice x1, local copies, waits for them, and re-layouts, body(): lax.dynamic_slice_in_dim(w_kv, head, 1, axis=3)  12.4 us

profile of v1, /device:TPU:0, one launch (start us, length us, event | category | flops | bytes accessed | tf_op | source)
XLA Modules:
  0.0 562.9 jit_solution(8255160165476592751)
XLA Ops:
  0.0 3.7 fusion
  3.7 1.9 pad_maximum_fusion.1
  5.7 12.4 %constant_dynamic-slice_fusion = bf16[2,3072,2,1,128]{4,3,2,1,0:T(2,128)(2,1)} fusion(bf16[2,3072,2,8,128]{4,3,2,1,0:T(8,128)(2,1)} %param.12, s32[]{:T(128)S(6)} %select_n.3), kind=kLoop, calls=%fused_computation.8 | loop fusion | bytes 6291460 | tf_op jit(solution)/shard_map/dynamic_slice | solution.py:411
  18.1 12.2 %copy.15 = bf16[2,3072,2,1,128]{1,4,2,0,3:T(8,128)(2,1)S(1)} copy(bf16[2,3072,2,1,128]{4,3,2,1,0:T(2,128)(2,1)} %constant_dynamic-slice_fusion) | data formatting | bytes 6291456
  30.4 2.8 copy.14
  33.2 6.6 %copy.11 = bf16[2,3072,3,128]{1,3,2,0:T(8,128)(2,1)} copy(bf16[2,3072,3,128]{3,1,2,0:T(8,128)(2,1)} %param.11) | data formatting | bytes 9437184 | tf_op args[2]
  39.8 0.0 copy-start
  39.8 6.8 %copy.13 = bf16[2,3072,384]{2,1,0:T(8,128)(2,1)} copy(bf16[2,3072,384]{1,2,0:T(8,128)(2,1)} %bitcast.7) | data formatting | bytes 9437184 | tf_op jit(solution)/shard_map/reshape | solution.py:412
  46.6 0.0 copy-done
  46.6 0.0 copy-start.1
  46.6 6.2 %pad_maximum_fusion.wqkv_h = bf16[2,3072,640]{2,1,0:T(8,128)(2,1)} fusion(bf16[2,3072,256]{2,1,0:T(8,128)(2,1)S(1)} %copy-done, bf16[2,3072,384]{2,1,0:T(8,128)(2,1)} %copy.13), kind=kLoop, calls=%fused_computation | loop fusion | flops 15728640 | bytes 15728640 | tf_op jit(solution)/shard_map/concatenate | solution.py:412
  52.8 0.0 copy-done.1
  52.8 0.6 fusion.2
  53.4 138.5 %attn0.1.r_ref = f32[256,3072]{1,0:T(8,128)} custom-call(bf16[256,3072]{1,0:T(8,128)(2,1)} %bitcast.10, f32[1,3072]{1,0:T(1,128)} %get-tuple-element.8.g_ref, f32[2048,128]{1,0:T(8,128)} %get-tuple-element.12.cos_ref, f32[2048,128]{1,0:T(8,128)} %get-tuple-element.13.sin_ref, bf16[2,3072,640]{2,1,0:T(8,128)(2,1)} %pad_maximum_fusion.wqkv_h, ...), custom_call_target="tpu_custom_call" | custom-call | tf_op jit(solution)/shard_map/attn0/pallas_call | solution.py:428
  191.9 1.4 fusion.1
  193.4 115.4 %mlp0.1.r_ref = f32[256,3072]{1,0:T(8,128)} custom-call(f32[256,3072]{1,0:T(8,128)} %attn0.1.r_ref, f32[1,3072]{1,0:T(1,128)} %get-tuple-element.6.g_ref, bf16[2,3072,1024]{2,1,0:T(8,128)(2,1)} %wg_h.3, bf16[2,3072,1024]{2,1,0:T(8,128)(2,1)} %wu_h.3, bf16[2,1024,3072]{2,1,0:T(8,128)(2,1)} %wd_h.3), custom_call_target="tpu_custom_call" | custom-call | tf_op jit(solution)/shard_map/mlp0/pallas_call | solution.py:430
  308.8 136.6 %attn1.1.r_ref = f32[256,3072]{1,0:T(8,128)} custom-call(f32[256,3072]{1,0:T(8,128)} %mlp0.1.r_ref, f32[1,3072]{1,0:T(1,128)} %get-tuple-element.7.g_ref, f32[2048,128]{1,0:T(8,128)} %get-tuple-element.12.cos_ref, f32[2048,128]{1,0:T(8,128)} %get-tuple-element.13.sin_ref, bf16[2,3072,640]{2,1,0:T(8,128)(2,1)} %pad_maximum_fusion.wqkv_h, ...), custom_call_target="tpu_custom_call" | custom-call | tf_op jit(solution)/shard_map/attn1/pallas_call | solution.py:428
  445.4 114.4 %mlp1.1 = bf16[256,3072]{1,0:T(8,128)(2,1)} custom-call(f32[256,3072]{1,0:T(8,128)} %attn1.1.r_ref, f32[1,3072]{1,0:T(1,128)} %get-tuple-element.5.g_ref, bf16[2,3072,1024]{2,1,0:T(8,128)(2,1)} %wg_h.3, bf16[2,3072,1024]{2,1,0:T(8,128)(2,1)} %wu_h.3, bf16[2,1024,3072]{2,1,0:T(8,128)(2,1)} %wd_h.3), custom_call_target="tpu_custom_call" | custom-call | tf_op jit(solution)/shard_map/mlp1/pallas_call | solution.py:430
  559.8 2.7 copy.17
  (2 shorter events, 0.0 us)
Async XLA Ops:
  39.8 6.8 %copy-start = (bf16[2,3072,256]{2,1,0:T(8,128)(2,1)S(1)}, bf16[2,3072,256]{2,1,0:T(8,128)(2,1)}, u32[]{:S(2)}) copy-start(bf16[2,3072,256]{2,1,0:T(8,128)(2,1)} %copy.14) | copy-start | bytes 9437188
  46.6 6.2 %copy-start.1 = (f32[2,3072]{1,0:T(2,128)S(1)}, f32[2,3072]{1,0:T(2,128)}, u32[]{:S(2)}) copy-start(f32[2,3072]{1,0:T(2,128)} %param.10) | copy-start | bytes 73732

commit v2 on v1

--- a/solution.py
+++ b/solution.py
@@ -1,6 +1,7 @@
 import functools
 import math
 import jax
+import numpy as np
 import jax.numpy as jnp
 from jax import lax
 from jax.experimental import pallas as pl
@@ -31,10 +32,12 @@
 
 
 def greet(pa, xn, yn):
-    barrier = pltpu.get_barrier_semaphore()
     for dev in (pa, xn, yn):
-        pl.semaphore_signal(barrier, inc=1, device_id={'tp': dev}, device_id_type=MESH)
-    pl.semaphore_wait(barrier, 3)
+        pl.semaphore_signal(pltpu.get_barrier_semaphore(), inc=1, device_id={'tp': dev}, device_id_type=MESH)
+
+
+def all_entered():
+    pl.semaphore_wait(pltpu.get_barrier_semaphore(), 3)
 
 
 def make_copies(G, PR, RX, RY, RD, S, ss, rs, pa, xn, yn):
@@ -80,7 +83,7 @@
         copies[name].wait_recv()
 
 
-def norm_rows(r_ref, g_ref, G):
+def norm_rows(layer, r_ref, g_ref, G):
     rows = r_ref.shape[0]
     step = 32
 
@@ -89,7 +92,7 @@
         at = pl.ds(pl.multiple_of(i * step, step), step)
         x = r_ref[at, :].astype(F32)
         mean_sq = jnp.mean(x * x, axis=-1, keepdims=True)
-        G[0, at, :] = (x * lax.rsqrt(mean_sq + EPS) * g_ref[...]).astype(BF16)
+        G[0, at, :] = (x * lax.rsqrt(mean_sq + EPS) * g_ref[layer:layer + 1, :]).astype(BF16)
 
 
 def finish(copies, r_ref, acc0, PR, RX, RY, o_ref):
@@ -152,82 +155,120 @@
                wg, wu, wd, G, PR, RX, RY, RD, S, acc0, acc7, u, ss, rs, ls):
     me, pa, dx, dy = places()
     xn, yn = me + dx, me + dy
+    greet(pa, xn, yn)
     loads = [pltpu.make_async_copy(h.at[layer], v, ls.at[i])
              for i, (h, v) in enumerate(((wg_h, wg), (wu_h, wu), (wd_h, wd)))]
     for load in loads:
         load.start()
-    norm_rows(r_ref, g_ref, G)
-    greet(pa, xn, yn)
+    norm_rows(layer, r_ref, g_ref, G)
+    all_entered()
     copies = make_copies(G, PR, RX, RY, RD, S, ss, rs, pa, xn, yn)
     to_partner, chip_sum, own, last = emitters(G, PR, S, acc0, acc7)
     start(copies, 'xh0', 'yh1', 'd1')
 
     def hidden(j):
         width = 256
-
-        @pl.loop(0, wg.shape[1] // width)
-        def _(n):
-            cols = pl.ds(pl.multiple_of(n * width, width), width)
-            gate = dot(G[j], wg[:, cols])
-            up = dot(G[j], wu[:, cols])
-            u[:, cols] = (jax.nn.silu(gate) * up).astype(BF16)
-
-    def tile(j, emit):
-        hidden(j)
-        project(u, wd, 512, emit)
+        blocks = wg.shape[1] // width
+
+        @pl.loop(0, 2 * blocks)
+        def _(i):
+            t = lax.div(i, blocks)
+            cols = pl.ds(pl.multiple_of(lax.rem(i, blocks) * width, width), width)
+            gate = dot(G[j + t], wg[:, cols])
+            up = dot(G[j + t], wu[:, cols])
+            u[t, :, cols] = (jax.nn.silu(gate) * up).astype(BF16)
+
+    def down(t, emit):
+        project(u.at[t], wd, 512, emit)
 
     for load in loads:
         load.wait()
-    tile(0, own)
     arrived(copies, 'd1')
-    tile(1, to_partner(1))
+    hidden(0)
+    down(1, to_partner(1))
     start(copies, 'p1')
     arrived(copies, 'xh0', 'yh1')
     start(copies, 'xf', 'yf', 'd2', 'xh1', 'yh0')
+    down(0, own)
     arrived(copies, 'd2')
-    tile(2, to_partner(2))
+    hidden(2)
+    down(0, to_partner(2))
     start(copies, 'p2')
     arrived(copies, 'p2')
-    tile(3, chip_sum(1, 0))
+    down(1, chip_sum(1, 0))
     start(copies, 'X0', 'Y1')
     arrived(copies, 'xf', 'yf')
     start(copies, 'd4')
     arrived(copies, 'd4')
-    tile(4, to_partner(4))
+    hidden(4)
+    down(0, to_partner(4))
     start(copies, 'p4')
     arrived(copies, 'p4')
-    tile(5, chip_sum(2, 1))
+    down(1, chip_sum(2, 1))
     start(copies, 'D0', 'D1')
     arrived(copies, 'xh1', 'yh0')
     start(copies, 'd6')
     arrived(copies, 'd6')
-    tile(6, to_partner(6))
+    hidden(6)
+    down(0, to_partner(6))
     start(copies, 'p6')
     arrived(copies, 'p6')
-    tile(7, last)
+    down(1, last)
     merge_last(copies, acc7, RD, S)
     finish(copies, r_ref, acc0, PR, RX, RY, o_ref)
 
 
-def attn_kernel(layer, head_dim, r_ref, g_ref, cos_ref, sin_ref, wqkv_h, wo_h, o_ref,
-                wqkv, wo, G, PR, RX, RY, RD, S, acc0, acc7, q_s, k_s, v_s, sc, l_s, ctx_acc, c_s, ss, rs, ls):
+def attn_kernel(layer, hd, n_kv, r_ref, g_ref, tab_ref, wq_h, wkv_h, wo_h, o_ref,
+                wqkv, wo, G, PR, RX, RY, RD, S, acc0, acc7, q_s, k_s, v_s, sc, l_s, ctx_acc, c_s,
+                proj, kv_in, kv_f, ss, rs, ls):
     me, pa, dx, dy = places()
     xn, yn = me + dx, me + dy
-    loads = [pltpu.make_async_copy(h.at[layer], v, ls.at[i])
-             for i, (h, v) in enumerate(((wqkv_h, wqkv), (wo_h, wo)))]
+    greet(pa, xn, yn)
+    rows = r_ref.shape[0]
+    half = rows // 2
+    group = wo.shape[0] // hd
+    chunk = sc.shape[2]
+    n_slots = q_s.shape[0]
+    kv_rows = kv_in.shape[1]
+    depth = kv_rows // (2 * n_kv)
+    n_parts = wqkv.shape[0] // depth
+
+    def kv_load(i, slot):
+        at = pl.ds(pl.multiple_of(i * kv_rows, kv_rows), kv_rows)
+        return pltpu.make_async_copy(wkv_h.at[layer, at], kv_in.at[slot], ls.at[slot])
+
+    kv_load(0, 0).start()
+    loads = [pltpu.make_async_copy(wq_h.at[layer, h], wqkv.at[:, h * hd:(h + 1) * hd], ls.at[3 + h])
+             for h in range(group)]
+    loads.append(pltpu.make_async_copy(wo_h.at[layer], wo, ls.at[2]))
     for load in loads:
         load.start()
-    norm_rows(r_ref, g_ref, G)
-    greet(pa, xn, yn)
+    norm_rows(layer, r_ref, g_ref, G)
+    all_entered()
     copies = make_copies(G, PR, RX, RY, RD, S, ss, rs, pa, xn, yn)
     to_partner, chip_sum, own, last = emitters(G, PR, S, acc0, acc7)
     start(copies, 'xh0', 'yh1', 'd1')
 
-    rows = r_ref.shape[0]
-    half = rows // 2
-    hd = head_dim
-    group = wo.shape[0] // hd
-    chunk = sc.shape[2]
+    @pl.loop(0, n_parts)
+    def _(i):
+        slot = lax.rem(i, 2)
+
+        @pl.when(i + 1 < n_parts)
+        def _():
+            kv_load(i + 1, 1 - slot).start()
+
+        kv_load(i, slot).wait()
+        piece = 512
+
+        @pl.loop(0, kv_rows // piece)
+        def _(n):
+            at = pl.ds(pl.multiple_of(n * piece, piece), piece)
+            kv_f[at, :] = kv_in[slot, at, :].astype(F32)
+
+        at = pl.ds(pl.multiple_of(i * depth, depth), depth)
+        for c in range(2):
+            picked = kv_f[pl.ds(me + c * n_kv, depth, stride=2 * n_kv), :]
+            wqkv[at, (group + c) * hd:(group + c + 1) * hd] = picked.astype(BF16)
 
     def halves(j):
         dev = me if j in (0, 3, 5, 7) else pa
@@ -242,22 +283,30 @@
         return first * rows, second * rows + half
 
     def qkv(j):
-        for hh, pos in enumerate(halves(j)):
-            pos = pl.multiple_of(pos, half)
+        proj[...] = dot(G[j], wqkv[...])
+        first, second = halves(j)
+
+        @pl.loop(0, 2)
+        def _(hh):
+            pos = pl.multiple_of(first + hh * (second - first), half)
+            slot = lax.div(pos, half)
             at = pl.ds(pos, half)
-            proj = dot(G[j, hh * half:(hh + 1) * half, :], wqkv[...])
-            cos_b = cos_ref[at, :]
-            sin_b = sin_ref[at, :]
+            out = pl.ds(pl.multiple_of(hh * half, half), half)
+            cos_a = tab_ref[pl.ds(slot, 1), :]
+            sin_a = tab_ref[pl.ds(n_slots + slot, 1), :]
+            base = 2 * n_slots
+            cos_o, sin_o, cos_n, sin_n = (tab_ref[base + n * half:base + (n + 1) * half, :] for n in range(4))
+            cos_b = cos_a * cos_o - sin_a * sin_o
+            sin_b = sin_a * cos_n + cos_a * sin_n
 
             def rope(n):
-                part = proj[:, n * hd:(n + 1) * hd]
+                part = proj[out, n * hd:(n + 1) * hd]
                 return (part * cos_b + pltpu.roll(part, hd // 2, 1) * sin_b).astype(BF16)
 
-            slot = lax.div(pos, half)
             for h in range(group):
                 q_s[slot, h * half:(h + 1) * half, :] = rope(h)
             k_s[at, :] = rope(group)
-            v_s[at, :] = proj[:, (group + 1) * hd:].astype(BF16)
+            v_s[at, :] = proj[out, (group + 1) * hd:].astype(BF16)
 
     scale = math.log2(math.e) / math.sqrt(hd)
 
@@ -311,9 +360,10 @@
         def _(hh):
             attend(pl.multiple_of(first + hh * (second - first), half), pl.multiple_of(hh * half, half))
 
-        project(c_s, wo, 512, emit)
-
-    loads[0].wait()
+        project(c_s, wo, 1024, emit)
+
+    for load in loads:
+        load.wait()
     qkv(0)
     arrived(copies, 'd1')
     qkv(1)
@@ -332,25 +382,24 @@
     qkv(7)
     arrived(copies, 'd6')
     qkv(6)
-    loads[1].wait()
-
+
+    tile(2, to_partner(2))
+    start(copies, 'p2')
+    arrived(copies, 'p2')
+    tile(3, chip_sum(1, 0))
+    start(copies, 'X0', 'Y1')
     tile(4, to_partner(4))
     start(copies, 'p4')
     arrived(copies, 'p4')
     tile(5, chip_sum(2, 1))
     start(copies, 'D0', 'D1')
-    tile(2, to_partner(2))
-    start(copies, 'p2')
-    arrived(copies, 'p2')
-    tile(3, chip_sum(1, 0))
-    start(copies, 'X0', 'Y1')
     tile(6, to_partner(6))
     start(copies, 'p6')
     arrived(copies, 'p6')
     tile(7, last)
-    merge_last(copies, acc7, RD, S)
     tile(1, to_partner(1))
     start(copies, 'p1')
+    merge_last(copies, acc7, RD, S)
     tile(0, own)
     finish(copies, r_ref, acc0, PR, RX, RY, o_ref)
 
@@ -387,12 +436,14 @@
     )
 
 
-def rope_tables(seq_len, head_dim):
-    half_dim = head_dim // 2
-    inv_freq = jnp.power(ROPE_BASE, -2.0 * jnp.arange(half_dim, dtype=F32) / head_dim)
-    angles = jnp.arange(seq_len).astype(F32)[:, None] * inv_freq[None, :]
-    cos_t, sin_t = jnp.cos(angles), jnp.sin(angles)
-    return jnp.concatenate([cos_t, cos_t], axis=1), jnp.concatenate([-sin_t, sin_t], axis=1)
+def rope_tables(seq_len, hd, half):
+    inv_freq = ROPE_BASE ** (-2.0 * np.arange(hd // 2) / hd)
+    inv_freq = np.concatenate([inv_freq, inv_freq])[None, :]
+    slots = half * np.arange(seq_len // half)[:, None] * inv_freq
+    offs = np.arange(half)[:, None] * inv_freq
+    sign = np.where(np.arange(hd) < hd // 2, -1.0, 1.0)[None, :]
+    rows = [np.cos(slots), np.sin(slots), np.cos(offs), np.sin(offs), sign * np.cos(offs), sign * np.sin(offs)]
+    return np.concatenate(rows).astype(np.float32)
 
 
 def solution(mesh):
@@ -406,29 +457,31 @@
         seq_len = rows * n_tp
         half = rows // 2
         ff = w_gate.shape[2]
-        chunk = 256
-        head = lax.axis_index('tp')
-        kv = lax.dynamic_slice_in_dim(w_kv, head, 1, axis=3).reshape(n_layers, width, 2 * hd)
-        wqkv = jnp.concatenate([w_q.reshape(n_layers, width, heads_loc * hd), kv], axis=2)
+        n_kv = w_kv.shape[3]
+        chunk = 512
+        kv_rows = 256 * 2 * n_kv
+        wq = jnp.transpose(w_q, (0, 2, 1, 3))
+        wkv = w_kv.reshape(n_layers, width * 2 * n_kv, hd)
         wo = w_o.reshape(n_layers, heads_loc * hd, width)
-        cos_t, sin_t = rope_tables(seq_len, hd)
+        tab = jnp.asarray(rope_tables(seq_len, hd, half))
         attn_scratch = [
-            pltpu.VMEM(wqkv.shape[1:], BF16), pltpu.VMEM(wo.shape[1:], BF16), *comm_scratch(rows, width),
+            pltpu.VMEM((width, (heads_loc + 2) * hd), BF16), pltpu.VMEM(wo.shape[1:], BF16), *comm_scratch(rows, width),
             pltpu.VMEM((seq_len // half, heads_loc * half, hd), BF16),
             pltpu.VMEM((seq_len, hd), BF16), pltpu.VMEM((seq_len, hd), BF16),
             pltpu.VMEM((seq_len // chunk, heads_loc * half, chunk), F32),
             pltpu.VMEM((heads_loc * half, hd), F32), pltpu.VMEM((heads_loc * half, hd), F32),
-            pltpu.VMEM((rows, heads_loc * hd), BF16), *semaphores(2)]
+            pltpu.VMEM((rows, heads_loc * hd), BF16), pltpu.VMEM((rows, (heads_loc + 2) * hd), F32),
+            pltpu.VMEM((2, kv_rows, hd), BF16), pltpu.VMEM((kv_rows, hd), F32), *semaphores(3 + heads_loc)]
         mlp_scratch = [
             pltpu.VMEM((width, ff), BF16), pltpu.VMEM((width, ff), BF16), pltpu.VMEM((ff, width), BF16),
-            *comm_scratch(rows, width), pltpu.VMEM((rows, ff), BF16), *semaphores(3)]
+            *comm_scratch(rows, width), pltpu.VMEM((2, rows, ff), BF16), *semaphores(3)]
         resid = hidden[0]
         for layer in range(n_layers):
             out_dtype = BF16 if layer == n_layers - 1 else F32
-            resid = call(functools.partial(attn_kernel, layer, hd), 2 * layer, F32, rows, width, 4, 2, attn_scratch, f'attn{layer}')(
-                resid, norm_attn[layer][None, :], cos_t, sin_t, wqkv, wo)
+            resid = call(functools.partial(attn_kernel, layer, hd, n_kv), 2 * layer, F32, rows, width, 3, 3, attn_scratch, f'attn{layer}')(
+                resid, norm_attn, tab, wq, wkv, wo)
             resid = call(functools.partial(mlp_kernel, layer), 2 * layer + 1, out_dtype, rows, width, 2, 3, mlp_scratch, f'mlp{layer}')(
-                resid, norm_mlp[layer][None, :], w_gate, w_up, w_down)
+                resid, norm_mlp, w_gate, w_up, w_down)
         return resid[None]
 
     return jax.shard_map(body, mesh=mesh, in_specs=in_specs, out_specs=tok_spec, check_vma=False)

time: 569 us -> 490 us (0.86)
  local copies, waits for them, and re-layouts: 45.6 us -> 2.65 us
  Pallas kernels: 505 us -> 479 us
  other arithmetic: 11.9 us -> 0 us
    unnamed x7 -> x1, local copies, waits for them, and re-layouts: 21.5 us -> 2.65 us
    pallas_call x2, Pallas kernels: 275 us -> 261 us  [body(): call(functools.partial(attn_kernel, layer, hd, n_kv), 2 * layer, F32, row...]
    dynamic_slice x1 -> x0, local copies, waits for them, and re-layouts: 12.4 us -> none  [body(): lax.dynamic_slice_in_dim(w_kv, head, 1, axis=3)]
    pallas_call x2, Pallas kernels: 230 us -> 218 us  [body(): call(functools.partial(mlp_kernel, layer), 2 * layer + 1, out_dtype, rows...]
    reshape x2 -> x0, local copies, waits for them, and re-layouts: 9.56 us -> none  [the longest x1 6.78 us: body(): w_q.reshape(n_layers, width, heads_loc * hd)]
    concatenate x2 -> x0, other arithmetic: 8.16 us -> none  [the longest x1 6.22 us: body(): jnp.concatenate([w_q.reshape(n_layers, width, heads_loc * hd), kv], axis=2)]
where the time goes in v2:
time: 490 us; the launch traced here: 482 us
  Pallas kernels  479 us (98%)
    pallas_call x2, Pallas kernels, body(): call(functools.partial(attn_kernel, layer, hd, n_kv), 2 * layer, F32, row...  261 us
    pallas_call x2, Pallas kernels, body(): call(functools.partial(mlp_kernel, layer), 2 * layer + 1, out_dtype, rows...  218 us

profile of v2, /device:TPU:0, one launch (start us, length us, event | category | flops | bytes accessed | tf_op | source)
XLA Modules:
  0.0 481.8 jit_solution(14525477046102430561)
XLA Ops:
  0.0 132.1 %attn0.1.r_ref = f32[256,3072]{1,0:T(8,128)} custom-call(bf16[256,3072]{1,0:T(8,128)(2,1)} %bitcast.12, f32[2,3072]{1,0:T(2,128)} %g_ref.6, f32[544,128]{1,0:T(8,128)} %constant.2.clone.tab_ref, bf16[2,3,3072,128]{3,2,1,0:T(8,128)(2,1)} %bitcast.7, bf16[2,49152,128]{2,1,0:T(8,128)(2,1)} %bitcast.5, bf16[2,384,3072]{2,1,0:T(8,128)(2,1)} %bitcast.9), custom_call_target="tpu_custom_call" | custom-call | tf_op jit(solution)/shard_map/attn0/pallas_call | solution.py:481
  132.1 108.8 %mlp0.1.r_ref = f32[256,3072]{1,0:T(8,128)} custom-call(f32[256,3072]{1,0:T(8,128)} %attn0.1.r_ref, f32[2,3072]{1,0:T(2,128)} %g_ref.7, bf16[2,3072,1024]{2,1,0:T(8,128)(2,1)} %wg_h.3, bf16[2,3072,1024]{2,1,0:T(8,128)(2,1)} %wu_h.3, bf16[2,1024,3072]{2,1,0:T(8,128)(2,1)} %wd_h.3), custom_call_target="tpu_custom_call" | custom-call | tf_op jit(solution)/shard_map/mlp0/pallas_call | solution.py:483
  240.9 128.9 %attn1.1.r_ref = f32[256,3072]{1,0:T(8,128)} custom-call(f32[256,3072]{1,0:T(8,128)} %mlp0.1.r_ref, f32[2,3072]{1,0:T(2,128)} %g_ref.6, f32[544,128]{1,0:T(8,128)} %constant.2.clone.tab_ref, bf16[2,3,3072,128]{3,2,1,0:T(8,128)(2,1)} %bitcast.8, bf16[2,49152,128]{2,1,0:T(8,128)(2,1)} %bitcast.6, bf16[2,384,3072]{2,1,0:T(8,128)(2,1)} %bitcast.10), custom_call_target="tpu_custom_call" | custom-call | tf_op jit(solution)/shard_map/attn1/pallas_call | solution.py:481
  369.8 108.9 %mlp1.1 = bf16[256,3072]{1,0:T(8,128)(2,1)} custom-call(f32[256,3072]{1,0:T(8,128)} %attn1.1.r_ref, f32[2,3072]{1,0:T(2,128)} %g_ref.7, bf16[2,3072,1024]{2,1,0:T(8,128)(2,1)} %wg_h.3, bf16[2,3072,1024]{2,1,0:T(8,128)(2,1)} %wu_h.3, bf16[2,1024,3072]{2,1,0:T(8,128)(2,1)} %wd_h.3), custom_call_target="tpu_custom_call" | custom-call | tf_op jit(solution)/shard_map/mlp1/pallas_call | solution.py:483
  478.7 2.7 copy.12

commit v3 on v2

--- a/solution.py
+++ b/solution.py
@@ -44,20 +44,20 @@
     half = G.shape[1] // 2
     lo, hi = pl.ds(0, half), pl.ds(half, half)
     table = {
-        'd1': (G.at[0], G.at[1], pa),
-        'xh0': (G.at[0, lo], G.at[3, lo], xn),
-        'yh1': (G.at[0, hi], G.at[3, hi], yn),
-        'xf': (G.at[3, hi], G.at[5, hi], xn),
-        'yf': (G.at[3, lo], G.at[5, lo], yn),
-        'xh1': (G.at[0, hi], G.at[7, lo], xn),
-        'yh0': (G.at[0, lo], G.at[7, hi], yn),
-        'd2': (G.at[3], G.at[2], pa),
-        'd4': (G.at[5], G.at[4], pa),
-        'd6': (G.at[7], G.at[6], pa),
+        'd0': (G.at[0], G.at[1], pa),
+        'xh0': (G.at[0, lo], G.at[2, lo], xn),
+        'yh1': (G.at[0, hi], G.at[2, hi], yn),
+        'xf': (G.at[2, hi], G.at[6, hi], xn),
+        'yf': (G.at[2, lo], G.at[6, lo], yn),
+        'xh1': (G.at[0, hi], G.at[4, lo], xn),
+        'yh0': (G.at[0, lo], G.at[4, hi], yn),
+        'd2': (G.at[2], G.at[3], pa),
+        'd4': (G.at[4], G.at[5], pa),
+        'd6': (G.at[6], G.at[7], pa),
         'p1': (G.at[1], PR.at[0], pa),
-        'p2': (G.at[2], PR.at[1], pa),
-        'p4': (G.at[4], PR.at[2], pa),
-        'p6': (G.at[6], PR.at[3], pa),
+        'p3': (G.at[3], PR.at[1], pa),
+        'p5': (G.at[5], PR.at[3], pa),
+        'p7': (G.at[7], PR.at[2], pa),
         'X0': (S.at[0, lo], RX.at[lo], xn),
         'Y1': (S.at[0, hi], RY.at[hi], yn),
         'D0': (S.at[1, lo], RD.at[hi], xn),
@@ -164,7 +164,7 @@
     all_entered()
     copies = make_copies(G, PR, RX, RY, RD, S, ss, rs, pa, xn, yn)
     to_partner, chip_sum, own, last = emitters(G, PR, S, acc0, acc7)
-    start(copies, 'xh0', 'yh1', 'd1')
+    start(copies, 'xh0', 'yh1', 'd0')
 
     def hidden(j):
         width = 256
@@ -183,7 +183,7 @@
 
     for load in loads:
         load.wait()
-    arrived(copies, 'd1')
+    arrived(copies, 'd0')
     hidden(0)
     down(1, to_partner(1))
     start(copies, 'p1')
@@ -192,34 +192,34 @@
     down(0, own)
     arrived(copies, 'd2')
     hidden(2)
-    down(0, to_partner(2))
-    start(copies, 'p2')
-    arrived(copies, 'p2')
-    down(1, chip_sum(1, 0))
+    down(1, to_partner(3))
+    start(copies, 'p3')
+    arrived(copies, 'p3')
+    down(0, chip_sum(1, 0))
     start(copies, 'X0', 'Y1')
     arrived(copies, 'xf', 'yf')
+    start(copies, 'd6')
+    arrived(copies, 'd6')
+    hidden(6)
+    down(1, to_partner(7))
+    start(copies, 'p7')
+    arrived(copies, 'p7')
+    down(0, chip_sum(2, 1))
+    start(copies, 'D0', 'D1')
+    arrived(copies, 'xh1', 'yh0')
     start(copies, 'd4')
     arrived(copies, 'd4')
     hidden(4)
-    down(0, to_partner(4))
-    start(copies, 'p4')
-    arrived(copies, 'p4')
-    down(1, chip_sum(2, 1))
-    start(copies, 'D0', 'D1')
-    arrived(copies, 'xh1', 'yh0')
-    start(copies, 'd6')
-    arrived(copies, 'd6')
-    hidden(6)
-    down(0, to_partner(6))
-    start(copies, 'p6')
-    arrived(copies, 'p6')
-    down(1, last)
+    down(1, to_partner(5))
+    start(copies, 'p5')
+    arrived(copies, 'p5')
+    down(0, last)
     merge_last(copies, acc7, RD, S)
     finish(copies, r_ref, acc0, PR, RX, RY, o_ref)
 
 
 def attn_kernel(layer, hd, n_kv, r_ref, g_ref, tab_ref, wq_h, wkv_h, wo_h, o_ref,
-                wqkv, wo, G, PR, RX, RY, RD, S, acc0, acc7, q_s, k_s, v_s, sc, l_s, ctx_acc, c_s,
+                wqkv, wo, G, PR, RX, RY, RD, S, acc0, acc7, q_s, k_s, v_s, top_s, sum_s, ctx_s, c_s,
                 proj, kv_in, kv_f, ss, rs, ls):
     me, pa, dx, dy = places()
     xn, yn = me + dx, me + dy
@@ -227,7 +227,7 @@
     rows = r_ref.shape[0]
     half = rows // 2
     group = wo.shape[0] // hd
-    chunk = sc.shape[2]
+    chunk = 2 * rows
     n_slots = q_s.shape[0]
     kv_rows = kv_in.shape[1]
     depth = kv_rows // (2 * n_kv)
@@ -247,7 +247,7 @@
     all_entered()
     copies = make_copies(G, PR, RX, RY, RD, S, ss, rs, pa, xn, yn)
     to_partner, chip_sum, own, last = emitters(G, PR, S, acc0, acc7)
-    start(copies, 'xh0', 'yh1', 'd1')
+    start(copies, 'xh0', 'yh1', 'd0', 'xh1', 'yh0')
 
     @pl.loop(0, n_parts)
     def _(i):
@@ -270,25 +270,20 @@
             picked = kv_f[pl.ds(me + c * n_kv, depth, stride=2 * n_kv), :]
             wqkv[at, (group + c) * hd:(group + c + 1) * hd] = picked.astype(BF16)
 
-    def halves(j):
-        dev = me if j in (0, 3, 5, 7) else pa
-        if j in (0, 1):
-            first, second = dev, dev
-        elif j in (4, 5):
-            first = second = dev + dx + dy
-        else:
-            first, second = dev + dx, dev + dy
-        if j in (6, 7):
-            return first * rows + half, second * rows
-        return first * rows, second * rows + half
-
-    def qkv(j):
-        proj[...] = dot(G[j], wqkv[...])
-        first, second = halves(j)
+    def position(i, t, hh):
+        dev = me + t * (pa - me)
+        far, diag = lax.div(i + 2, 3), lax.div(i, 3)
+        swap = lax.div(i, 2) - diag
+        first = (dev + far * dx + diag * dy) * rows + swap * half
+        second = (dev + far * dy + diag * dx) * rows + (1 - swap) * half
+        return pl.multiple_of(first + hh * (second - first), half)
+
+    def qkv(i, t):
+        proj[...] = dot(G[2 * i + t], wqkv[...])
 
         @pl.loop(0, 2)
         def _(hh):
-            pos = pl.multiple_of(first + hh * (second - first), half)
+            pos = position(i, t, hh)
             slot = lax.div(pos, half)
             at = pl.ds(pos, half)
             out = pl.ds(pl.multiple_of(hh * half, half), half)
@@ -310,9 +305,8 @@
 
     scale = math.log2(math.e) / math.sqrt(hd)
 
-    def scores(q, start_key):
-        keys = k_s[pl.ds(start_key, chunk), :]
-        return lax.dot_general(q, keys, (((1,), (1,)), ((), ())), preferred_element_type=F32)
+    def scores(q, keys):
+        return lax.dot_general(q, k_s[keys, :], (((1,), (1,)), ((), ())), preferred_element_type=F32)
 
     def fold(s, op):
         out = s[:, :hd]
@@ -320,87 +314,130 @@
             out = op(out, s[:, n * hd:(n + 1) * hd])
         return out
 
-    def attend(pos, out_row):
-        q = q_s[lax.div(pos, half)]
-        n_full = lax.div(pos, chunk)
-        edge = pl.multiple_of(n_full * chunk, chunk)
-        s = scores(q, edge)
+    def reset(st):
+        top_s[st] = jnp.full(top_s.shape[1:], -jnp.inf, F32)
+        sum_s[st] = jnp.zeros(sum_s.shape[1:], F32)
+        ctx_s[st] = jnp.zeros(ctx_s.shape[1:], F32)
+
+    def absorb(st, pos, c):
+        keys = pl.ds(pl.multiple_of(c * chunk, chunk), chunk)
+        s = scores(q_s[lax.div(pos, half)], keys)
         shape = (half, chunk)
-        row = lax.broadcasted_iota(jnp.int32, shape, 0) + (pos - edge)
+        row = lax.broadcasted_iota(jnp.int32, shape, 0) + (pos - c * chunk)
         keep = lax.broadcasted_iota(jnp.int32, shape, 1) <= row
-        keep = jnp.concatenate([keep] * group, axis=0)
-        s = jnp.where(keep, s, -jnp.inf)
-        sc[n_full] = s
-        l_s[...] = fold(s, jnp.maximum)
-
-        @pl.loop(0, n_full)
-        def _(c):
-            s = scores(q, pl.multiple_of(c * chunk, chunk))
-            sc[c] = s
-            l_s[...] = jnp.maximum(l_s[...], fold(s, jnp.maximum))
-
-        top = jnp.max(l_s[...], axis=1, keepdims=True)
-        l_s[...] = jnp.zeros_like(l_s)
-        ctx_acc[...] = jnp.zeros_like(ctx_acc)
-
-        @pl.loop(0, n_full + 1)
-        def _(c):
-            p = jnp.exp2((sc[c] - top) * scale)
-            l_s[...] += fold(p, jnp.add)
-            ctx_acc[...] += dot(p.astype(BF16), v_s[pl.ds(pl.multiple_of(c * chunk, chunk), chunk), :])
-
-        out = (ctx_acc[...] / jnp.sum(l_s[...], axis=1, keepdims=True)).astype(BF16)
+        s = jnp.where(jnp.concatenate([keep] * group, axis=0), s, -jnp.inf)
+        old = top_s[st]
+        top = jnp.maximum(old, jnp.max(fold(s, jnp.maximum), axis=1, keepdims=True))
+        top_s[st] = top
+        shrink = jnp.exp2((old - top) * scale)
+        p = jnp.exp2((s - top[:, :1]) * scale)
+        sum_s[st] = sum_s[st] * shrink + fold(p, jnp.add)
+        ctx_s[st] = ctx_s[st] * shrink + dot(p.astype(BF16), v_s[keys, :])
+
+    def settle(st, hh):
+        out = (ctx_s[st] / jnp.sum(sum_s[st], axis=1, keepdims=True)).astype(BF16)
+        at = pl.ds(pl.multiple_of(hh * half, half), half)
         for h in range(group):
-            c_s[pl.ds(out_row, half), h * hd:(h + 1) * hd] = out[h * half:(h + 1) * half, :]
-
-    def tile(j, emit):
-        first, second = halves(j)
-
+            c_s[at, h * hd:(h + 1) * hd] = out[h * half:(h + 1) * half, :]
+
+    chip = lax.div(me, 2)
+    dx_chip, dy_chip = lax.div(dx, 2), lax.div(dy, 2)
+
+    def early():
+        @pl.loop(0, 4)
+        def _(st):
+            pos = position(1, 1 - lax.div(st, 2), lax.rem(st, 2))
+            reset(st)
+
+            @pl.loop(0, 3)
+            def _(n):
+                c = chip + lax.rem(n, 2) * dx_chip + lax.div(n, 2) * dy_chip
+
+                @pl.when(c <= lax.div(pos, chunk))
+                def _():
+                    absorb(st, pos, c)
+
+    def emit_pair(n, name, emit_partner, emit_own):
+        @pl.when(n == 0)
+        def _():
+            project(c_s, wo, 1024, emit_partner)
+            start(copies, name)
+
+        @pl.when(n == 1)
+        def _():
+            if emit_own is not own:
+                arrived(copies, name)
+            project(c_s, wo, 1024, emit_own)
+
+    def first_pair(name, emit_partner, emit_own):
         @pl.loop(0, 2)
-        def _(hh):
-            attend(pl.multiple_of(first + hh * (second - first), half), pl.multiple_of(hh * half, half))
-
-        project(c_s, wo, 1024, emit)
+        def _(n):
+            @pl.loop(0, 2)
+            def _(hh):
+                pos = position(1, 1 - n, hh)
+                c = chip + dx_chip + dy_chip
+
+                @pl.when(c <= lax.div(pos, chunk))
+                def _():
+                    absorb(2 * n + hh, pos, c)
+
+                settle(2 * n + hh, hh)
+
+            emit_pair(n, name, emit_partner, emit_own)
+
+    def pair(i, name, emit_partner, emit_own):
+        @pl.loop(0, 2)
+        def _(n):
+            @pl.loop(0, 2)
+            def _(hh):
+                pos = position(i, 1 - n, hh)
+                reset(0)
+
+                @pl.loop(0, lax.div(pos, chunk) + 1)
+                def _(c):
+                    absorb(0, pos, c)
+
+                settle(0, hh)
+
+            emit_pair(n, name, emit_partner, emit_own)
 
     for load in loads:
         load.wait()
-    qkv(0)
-    arrived(copies, 'd1')
-    qkv(1)
-    arrived(copies, 'xh0', 'yh1')
-    start(copies, 'xf', 'yf', 'd2', 'xh1', 'yh0')
-    qkv(3)
-    arrived(copies, 'd2')
-    qkv(2)
-    arrived(copies, 'xf', 'yf')
-    start(copies, 'd4')
-    qkv(5)
-    arrived(copies, 'd4')
-    qkv(4)
-    arrived(copies, 'xh1', 'yh0')
-    start(copies, 'd6')
-    qkv(7)
-    arrived(copies, 'd6')
-    qkv(6)
-
-    tile(2, to_partner(2))
-    start(copies, 'p2')
-    arrived(copies, 'p2')
-    tile(3, chip_sum(1, 0))
+
+    @pl.loop(0, 4)
+    def _(i):
+        @pl.when(i == 1)
+        def _():
+            arrived(copies, 'xh0', 'yh1')
+            start(copies, 'xf', 'yf', 'd2')
+
+        @pl.when(i == 2)
+        def _():
+            arrived(copies, 'xh1', 'yh0')
+            start(copies, 'd4')
+
+        @pl.when(i == 3)
+        def _():
+            early()
+            arrived(copies, 'xf', 'yf')
+            start(copies, 'd6')
+
+        @pl.loop(0, 2)
+        def _(t):
+            for n, name in enumerate(('d0', 'd2', 'd4', 'd6')):
+                @pl.when((t == 1) & (i == n))
+                def _(name=name):
+                    arrived(copies, name)
+
+            qkv(i, t)
+
+    first_pair('p3', to_partner(3), chip_sum(1, 0))
     start(copies, 'X0', 'Y1')
-    tile(4, to_partner(4))
-    start(copies, 'p4')
-    arrived(copies, 'p4')
-    tile(5, chip_sum(2, 1))
+    pair(3, 'p7', to_partner(7), chip_sum(2, 1))
     start(copies, 'D0', 'D1')
-    tile(6, to_partner(6))
-    start(copies, 'p6')
-    arrived(copies, 'p6')
-    tile(7, last)
-    tile(1, to_partner(1))
-    start(copies, 'p1')
+    pair(2, 'p5', to_partner(5), last)
+    pair(0, 'p1', to_partner(1), own)
     merge_last(copies, acc7, RD, S)
-    tile(0, own)
     finish(copies, r_ref, acc0, PR, RX, RY, o_ref)
 
 
@@ -458,7 +495,6 @@
         half = rows // 2
         ff = w_gate.shape[2]
         n_kv = w_kv.shape[3]
-        chunk = 512
         kv_rows = 256 * 2 * n_kv
         wq = jnp.transpose(w_q, (0, 2, 1, 3))
         wkv = w_kv.reshape(n_layers, width * 2 * n_kv, hd)
@@ -468,8 +504,7 @@
             pltpu.VMEM((width, (heads_loc + 2) * hd), BF16), pltpu.VMEM(wo.shape[1:], BF16), *comm_scratch(rows, width),
             pltpu.VMEM((seq_len // half, heads_loc * half, hd), BF16),
             pltpu.VMEM((seq_len, hd), BF16), pltpu.VMEM((seq_len, hd), BF16),
-            pltpu.VMEM((seq_len // chunk, heads_loc * half, chunk), F32),
-            pltpu.VMEM((heads_loc * half, hd), F32), pltpu.VMEM((heads_loc * half, hd), F32),
+            *[pltpu.VMEM((4, heads_loc * half, hd), F32)] * 3,
             pltpu.VMEM((rows, heads_loc * hd), BF16), pltpu.VMEM((rows, (heads_loc + 2) * hd), F32),
             pltpu.VMEM((2, kv_rows, hd), BF16), pltpu.VMEM((kv_rows, hd), F32), *semaphores(3 + heads_loc)]
         mlp_scratch = [

time: 490 us -> 472 us (0.963); the launches traced: 482 us -> 472 us
  Pallas kernels: 479 us -> 469 us
    pallas_call x2, Pallas kernels: 261 us -> 246 us  [body(): call(functools.partial(attn_kernel, layer, hd, n_kv), 2 * layer, F32, row...]
    pallas_call x2, Pallas kernels: 218 us -> 223 us  [body(): call(functools.partial(mlp_kernel, layer), 2 * layer + 1, out_dtype, rows...]
where the time goes in v3:
time: 472 us
  Pallas kernels  469 us (99%)
    pallas_call x2, Pallas kernels, body(): call(functools.partial(attn_kernel, layer, hd, n_kv), 2 * layer, F32, row...  246 us
    pallas_call x2, Pallas kernels, body(): call(functools.partial(mlp_kernel, layer), 2 * layer + 1, out_dtype, rows...  223 us

profile of v3, /device:TPU:0, one launch (start us, length us, event | category | flops | bytes accessed | tf_op | source)
XLA Modules:
  0.0 471.7 jit_solution(16389892480198086135)
XLA Ops:
  0.0 124.3 %attn0.1.r_ref = f32[256,3072]{1,0:T(8,128)} custom-call(bf16[256,3072]{1,0:T(8,128)(2,1)} %bitcast.12, f32[2,3072]{1,0:T(2,128)} %g_ref.6, f32[544,128]{1,0:T(8,128)} %constant.2.clone.tab_ref, bf16[2,3,3072,128]{3,2,1,0:T(8,128)(2,1)} %bitcast.7, bf16[2,49152,128]{2,1,0:T(8,128)(2,1)} %bitcast.5, bf16[2,384,3072]{2,1,0:T(8,128)(2,1)} %bitcast.9), custom_call_target="tpu_custom_call" | custom-call | tf_op jit(solution)/shard_map/attn0/pallas_call | solution.py:516
  124.3 110.1 %mlp0.1.r_ref = f32[256,3072]{1,0:T(8,128)} custom-call(f32[256,3072]{1,0:T(8,128)} %attn0.1.r_ref, f32[2,3072]{1,0:T(2,128)} %g_ref.7, bf16[2,3072,1024]{2,1,0:T(8,128)(2,1)} %wg_h.3, bf16[2,3072,1024]{2,1,0:T(8,128)(2,1)} %wu_h.3, bf16[2,1024,3072]{2,1,0:T(8,128)(2,1)} %wd_h.3), custom_call_target="tpu_custom_call" | custom-call | tf_op jit(solution)/shard_map/mlp0/pallas_call | solution.py:518
  234.5 122.1 %attn1.1.r_ref = f32[256,3072]{1,0:T(8,128)} custom-call(f32[256,3072]{1,0:T(8,128)} %mlp0.1.r_ref, f32[2,3072]{1,0:T(2,128)} %g_ref.6, f32[544,128]{1,0:T(8,128)} %constant.2.clone.tab_ref, bf16[2,3,3072,128]{3,2,1,0:T(8,128)(2,1)} %bitcast.8, bf16[2,49152,128]{2,1,0:T(8,128)(2,1)} %bitcast.6, bf16[2,384,3072]{2,1,0:T(8,128)(2,1)} %bitcast.10), custom_call_target="tpu_custom_call" | custom-call | tf_op jit(solution)/shard_map/attn1/pallas_call | solution.py:516
  356.5 112.5 %mlp1.1 = bf16[256,3072]{1,0:T(8,128)(2,1)} custom-call(f32[256,3072]{1,0:T(8,128)} %attn1.1.r_ref, f32[2,3072]{1,0:T(2,128)} %g_ref.7, bf16[2,3072,1024]{2,1,0:T(8,128)(2,1)} %wg_h.3, bf16[2,3072,1024]{2,1,0:T(8,128)(2,1)} %wu_h.3, bf16[2,1024,3072]{2,1,0:T(8,128)(2,1)} %wd_h.3), custom_call_target="tpu_custom_call" | custom-call | tf_op jit(solution)/shard_map/mlp1/pallas_call | solution.py:518
  469.0 2.7 copy.12

commit v4 on v3

--- a/solution.py
+++ b/solution.py
@@ -83,29 +83,33 @@
         copies[name].wait_recv()
 
 
-def norm_rows(layer, r_ref, g_ref, G):
-    rows = r_ref.shape[0]
+def normed(x, gain):
+    mean_sq = jnp.mean(x * x, axis=-1, keepdims=True)
+    return (x * lax.rsqrt(mean_sq + EPS) * gain).astype(BF16)
+
+
+def norm_rows(r_s, gain_ref, G):
     step = 32
 
-    @pl.loop(0, rows // step)
+    @pl.loop(0, r_s.shape[0] // step)
     def _(i):
         at = pl.ds(pl.multiple_of(i * step, step), step)
-        x = r_ref[at, :].astype(F32)
-        mean_sq = jnp.mean(x * x, axis=-1, keepdims=True)
-        G[0, at, :] = (x * lax.rsqrt(mean_sq + EPS) * g_ref[layer:layer + 1, :]).astype(BF16)
-
-
-def finish(copies, r_ref, acc0, PR, RX, RY, o_ref):
+        G[0, at, :] = normed(r_s[at, :].astype(F32), gain_ref[...])
+
+
+def finish(copies, r_s, acc0, PR, RX, RY, o_ref, next_ref, gain_ref):
     arrived(copies, 'p1', 'X0', 'X1', 'Y0', 'Y1')
-    rows = r_ref.shape[0]
     step = 32
 
-    @pl.loop(0, rows // step)
+    @pl.loop(0, r_s.shape[0] // step)
     def _(i):
         at = pl.ds(pl.multiple_of(i * step, step), step)
         total = acc0[at, :] + PR[0, at, :].astype(F32)
         total += RX[at, :].astype(F32) + RY[at, :].astype(F32)
-        o_ref[at, :] = (r_ref[at, :].astype(F32) + total).astype(o_ref.dtype)
+        x = r_s[at, :].astype(F32) + total
+        o_ref[at, :] = x.astype(o_ref.dtype)
+        if next_ref is not None:
+            next_ref[at, :] = normed(x, gain_ref[...])
 
     for copy in copies.values():
         copy.wait_send()
@@ -151,20 +155,30 @@
     return to_partner, chip_sum, own, last
 
 
-def mlp_kernel(layer, r_ref, g_ref, wg_h, wu_h, wd_h, o_ref,
-               wg, wu, wd, G, PR, RX, RY, RD, S, acc0, acc7, u, ss, rs, ls):
+def mlp_kernel(layer, last_layer, r_h, a_h, na_ref, nm_ref, wg_h, wu_h, wd_h, o_ref, *refs):
+    if last_layer:
+        next_ref, gain_ref, acc0 = None, None, refs[-1]
+        refs = refs[:-1]
+    else:
+        next_ref, gain_ref, acc0 = refs[0], na_ref.at[layer + 1:layer + 2], o_ref
+        refs = refs[1:]
+    wg, wu, wd, u, r_s, G, PR, RX, RY, RD, S, acc7, ss, rs, ls = refs
     me, pa, dx, dy = places()
     xn, yn = me + dx, me + dy
     greet(pa, xn, yn)
     loads = [pltpu.make_async_copy(h.at[layer], v, ls.at[i])
              for i, (h, v) in enumerate(((wg_h, wg), (wu_h, wu), (wd_h, wd)))]
-    for load in loads:
-        load.start()
-    norm_rows(layer, r_ref, g_ref, G)
+    rows_in = pltpu.make_async_copy(a_h, G.at[0], ls.at[3])
+    resid_in = pltpu.make_async_copy(r_h, r_s, ls.at[4])
+    rows_in.start()
+    rows_in.wait()
     all_entered()
     copies = make_copies(G, PR, RX, RY, RD, S, ss, rs, pa, xn, yn)
     to_partner, chip_sum, own, last = emitters(G, PR, S, acc0, acc7)
     start(copies, 'xh0', 'yh1', 'd0')
+    for load in loads:
+        load.start()
+    resid_in.start()
 
     def hidden(j):
         width = 256
@@ -215,16 +229,18 @@
     arrived(copies, 'p5')
     down(0, last)
     merge_last(copies, acc7, RD, S)
-    finish(copies, r_ref, acc0, PR, RX, RY, o_ref)
-
-
-def attn_kernel(layer, hd, n_kv, r_ref, g_ref, tab_ref, wq_h, wkv_h, wo_h, o_ref,
-                wqkv, wo, G, PR, RX, RY, RD, S, acc0, acc7, q_s, k_s, v_s, top_s, sum_s, ctx_s, c_s,
-                proj, kv_in, kv_f, ss, rs, ls):
+    resid_in.wait()
+    finish(copies, r_s, acc0, PR, RX, RY, o_ref, next_ref, gain_ref)
+
+
+def attn_kernel(layer, hd, n_kv, r_h, a_h, na_ref, nm_ref, tab_ref, wq_h, wkv_h, wo_h, o_ref, next_ref,
+                wqkv, wo, q_s, k_s, v_s, top_s, sum_s, ctx_s, c_s, proj, kv_in, kv_f,
+                r_s, G, PR, RX, RY, RD, S, acc7, ss, rs, ls):
+    acc0 = o_ref
     me, pa, dx, dy = places()
     xn, yn = me + dx, me + dy
     greet(pa, xn, yn)
-    rows = r_ref.shape[0]
+    rows = r_s.shape[0]
     half = rows // 2
     group = wo.shape[0] // hd
     chunk = 2 * rows
@@ -237,17 +253,26 @@
         at = pl.ds(pl.multiple_of(i * kv_rows, kv_rows), kv_rows)
         return pltpu.make_async_copy(wkv_h.at[layer, at], kv_in.at[slot], ls.at[slot])
 
-    kv_load(0, 0).start()
+    resid_in = pltpu.make_async_copy(r_h, r_s, ls.at[3 + group])
+    rows_in = resid_in
+    if layer > 0:
+        rows_in = pltpu.make_async_copy(a_h, G.at[0], ls.at[4 + group])
+    rows_in.start()
     loads = [pltpu.make_async_copy(wq_h.at[layer, h], wqkv.at[:, h * hd:(h + 1) * hd], ls.at[3 + h])
              for h in range(group)]
     loads.append(pltpu.make_async_copy(wo_h.at[layer], wo, ls.at[2]))
-    for load in loads:
-        load.start()
-    norm_rows(layer, r_ref, g_ref, G)
+    rows_in.wait()
+    if layer == 0:
+        norm_rows(r_s, na_ref.at[layer:layer + 1], G)
     all_entered()
     copies = make_copies(G, PR, RX, RY, RD, S, ss, rs, pa, xn, yn)
     to_partner, chip_sum, own, last = emitters(G, PR, S, acc0, acc7)
     start(copies, 'xh0', 'yh1', 'd0', 'xh1', 'yh0')
+    kv_load(0, 0).start()
+    for load in loads:
+        load.start()
+    if layer > 0:
+        resid_in.start()
 
     @pl.loop(0, n_parts)
     def _(i):
@@ -278,30 +303,36 @@
         second = (dev + far * dy + diag * dx) * rows + (1 - swap) * half
         return pl.multiple_of(first + hh * (second - first), half)
 
-    def qkv(i, t):
-        proj[...] = dot(G[2 * i + t], wqkv[...])
+    def turn(part, slot):
+        cos_a = tab_ref[pl.ds(slot, 1), :]
+        sin_a = tab_ref[pl.ds(n_slots + slot, 1), :]
+        base = 2 * n_slots
+        cos_o, sin_o, cos_n, sin_n = (tab_ref[base + n * half:base + (n + 1) * half, :] for n in range(4))
+        cos_b = cos_a * cos_o - sin_a * sin_o
+        sin_b = sin_a * cos_n + cos_a * sin_n
+        return (part * cos_b + pltpu.roll(part, hd // 2, 1) * sin_b).astype(BF16)
+
+    q_cols, kv_cols = pl.ds(0, group * hd), pl.ds(group * hd, 2 * hd)
+
+    def keys_values(i, t):
+        proj[:, kv_cols] = dot(G[2 * i + t], wqkv[:, kv_cols])
 
         @pl.loop(0, 2)
         def _(hh):
             pos = position(i, t, hh)
-            slot = lax.div(pos, half)
-            at = pl.ds(pos, half)
             out = pl.ds(pl.multiple_of(hh * half, half), half)
-            cos_a = tab_ref[pl.ds(slot, 1), :]
-            sin_a = tab_ref[pl.ds(n_slots + slot, 1), :]
-            base = 2 * n_slots
-            cos_o, sin_o, cos_n, sin_n = (tab_ref[base + n * half:base + (n + 1) * half, :] for n in range(4))
-            cos_b = cos_a * cos_o - sin_a * sin_o
-            sin_b = sin_a * cos_n + cos_a * sin_n
-
-            def rope(n):
-                part = proj[out, n * hd:(n + 1) * hd]
-                return (part * cos_b + pltpu.roll(part, hd // 2, 1) * sin_b).astype(BF16)
-
+            k_s[pl.ds(pos, half), :] = turn(proj[out, group * hd:(group + 1) * hd], lax.div(pos, half))
+            v_s[pl.ds(pos, half), :] = proj[out, (group + 1) * hd:].astype(BF16)
+
+    def queries(i, t):
+        proj[:, q_cols] = dot(G[2 * i + t], wqkv[:, q_cols])
+
+        @pl.loop(0, 2)
+        def _(hh):
+            slot = lax.div(position(i, t, hh), half)
+            out = pl.ds(pl.multiple_of(hh * half, half), half)
             for h in range(group):
-                q_s[slot, h * half:(h + 1) * half, :] = rope(h)
-            k_s[at, :] = rope(group)
-            v_s[at, :] = proj[out, (group + 1) * hd:].astype(BF16)
+                q_s[slot, h * half:(h + 1) * half, :] = turn(proj[out, h * hd:(h + 1) * hd], slot)
 
     scale = math.log2(math.e) / math.sqrt(hd)
 
@@ -429,20 +460,32 @@
                 def _(name=name):
                     arrived(copies, name)
 
-            qkv(i, t)
+            keys_values(i, t)
+
+            @pl.when(i < 3)
+            def _():
+                queries(i, t)
 
     first_pair('p3', to_partner(3), chip_sum(1, 0))
     start(copies, 'X0', 'Y1')
+
+    @pl.loop(0, 2)
+    def _(t):
+        queries(3, t)
+
     pair(3, 'p7', to_partner(7), chip_sum(2, 1))
     start(copies, 'D0', 'D1')
     pair(2, 'p5', to_partner(5), last)
     pair(0, 'p1', to_partner(1), own)
     merge_last(copies, acc7, RD, S)
-    finish(copies, r_ref, acc0, PR, RX, RY, o_ref)
-
-
-def comm_scratch(rows, width):
+    if layer > 0:
+        resid_in.wait()
+    finish(copies, r_s, acc0, PR, RX, RY, o_ref, next_ref, nm_ref.at[layer:layer + 1])
+
+
+def comm_scratch(rows, width, n_loads, resid_dtype):
     return [
+        pltpu.VMEM((rows, width), resid_dtype),
         pltpu.VMEM((8, rows, width), BF16),
         pltpu.VMEM((4, rows, width), BF16),
         pltpu.VMEM((rows, width), BF16),
@@ -450,22 +493,19 @@
         pltpu.VMEM((rows, width), BF16),
         pltpu.VMEM((3, rows, width), BF16),
         pltpu.VMEM((rows, width), F32),
-        pltpu.VMEM((rows, width), F32),
+        pltpu.SemaphoreType.DMA((N_COPIES,)),
+        pltpu.SemaphoreType.DMA((N_COPIES,)),
+        pltpu.SemaphoreType.DMA((n_loads,)),
     ]
 
 
-def semaphores(n_loads):
-    return [pltpu.SemaphoreType.DMA((N_COPIES,)), pltpu.SemaphoreType.DMA((N_COPIES,)),
-            pltpu.SemaphoreType.DMA((n_loads,))]
-
-
-def call(kernel, collective, out_dtype, rows, width, n_vmem, n_any, scratch, name):
-    vmem = pl.BlockSpec(memory_space=pltpu.VMEM)
+def call(kernel, collective, shapes, n_vmem, n_any, scratch, name):
+    vmem, anywhere = pl.BlockSpec(memory_space=pltpu.VMEM), pl.BlockSpec(memory_space=pl.ANY)
     return pl.pallas_call(
         kernel,
-        out_shape=jax.ShapeDtypeStruct((rows, width), out_dtype),
-        in_specs=[vmem] * n_vmem + [pl.BlockSpec(memory_space=pl.ANY)] * n_any,
-        out_specs=vmem,
+        out_shape=shapes,
+        in_specs=[anywhere] * 2 + [vmem] * n_vmem + [anywhere] * n_any,
+        out_specs=[vmem] * len(shapes),
         scratch_shapes=scratch,
         compiler_params=pltpu.CompilerParams(
             collective_id=collective, has_side_effects=True, vmem_limit_bytes=VMEM_LIMIT),
@@ -501,22 +541,28 @@
         wo = w_o.reshape(n_layers, heads_loc * hd, width)
         tab = jnp.asarray(rope_tables(seq_len, hd, half))
         attn_scratch = [
-            pltpu.VMEM((width, (heads_loc + 2) * hd), BF16), pltpu.VMEM(wo.shape[1:], BF16), *comm_scratch(rows, width),
+            pltpu.VMEM((width, (heads_loc + 2) * hd), BF16), pltpu.VMEM(wo.shape[1:], BF16),
             pltpu.VMEM((seq_len // half, heads_loc * half, hd), BF16),
             pltpu.VMEM((seq_len, hd), BF16), pltpu.VMEM((seq_len, hd), BF16),
             *[pltpu.VMEM((4, heads_loc * half, hd), F32)] * 3,
             pltpu.VMEM((rows, heads_loc * hd), BF16), pltpu.VMEM((rows, (heads_loc + 2) * hd), F32),
-            pltpu.VMEM((2, kv_rows, hd), BF16), pltpu.VMEM((kv_rows, hd), F32), *semaphores(3 + heads_loc)]
+            pltpu.VMEM((2, kv_rows, hd), BF16), pltpu.VMEM((kv_rows, hd), F32)]
         mlp_scratch = [
             pltpu.VMEM((width, ff), BF16), pltpu.VMEM((width, ff), BF16), pltpu.VMEM((ff, width), BF16),
-            *comm_scratch(rows, width), pltpu.VMEM((2, rows, ff), BF16), *semaphores(3)]
-        resid = hidden[0]
+            pltpu.VMEM((2, rows, ff), BF16), *comm_scratch(rows, width, 5, F32)]
+        both = [jax.ShapeDtypeStruct((rows, width), F32), jax.ShapeDtypeStruct((rows, width), BF16)]
+        resid = following = hidden[0]
         for layer in range(n_layers):
-            out_dtype = BF16 if layer == n_layers - 1 else F32
-            resid = call(functools.partial(attn_kernel, layer, hd, n_kv), 2 * layer, F32, rows, width, 3, 3, attn_scratch, f'attn{layer}')(
-                resid, norm_attn, tab, wq, wkv, wo)
-            resid = call(functools.partial(mlp_kernel, layer), 2 * layer + 1, out_dtype, rows, width, 2, 3, mlp_scratch, f'mlp{layer}')(
-                resid, norm_mlp, w_gate, w_up, w_down)
+            last_layer = layer == n_layers - 1
+            resid, following = call(
+                functools.partial(attn_kernel, layer, hd, n_kv), 2 * layer, both, 3, 3,
+                attn_scratch + comm_scratch(rows, width, 5 + heads_loc, resid.dtype), f'attn{layer}')(
+                resid, following, norm_attn, norm_mlp, tab, wq, wkv, wo)
+            resid, *following = call(
+                functools.partial(mlp_kernel, layer, last_layer), 2 * layer + 1, both[1:] if last_layer else both, 2, 3,
+                mlp_scratch + [pltpu.VMEM((rows, width), F32)] * last_layer, f'mlp{layer}')(
+                resid, following, norm_attn, norm_mlp, w_gate, w_up, w_down)
+            following = following[0] if following else None
         return resid[None]
 
     return jax.shard_map(body, mesh=mesh, in_specs=in_specs, out_specs=tok_spec, check_vma=False)

time: 472 us -> 480 us (1.017)
  Pallas kernels: 469 us -> 476 us
    pallas_call x4, Pallas kernels: 469 us -> 476 us  [the longest x2 252 us: body(): call(functools.partial(attn_kernel, layer, hd, n_kv), 2 * layer, both, 3,...]
where the time goes in v4:
time: 480 us; the launch traced here: 479 us
  Pallas kernels  476 us (99%)
    pallas_call x2, Pallas kernels, body(): call(functools.partial(attn_kernel, layer, hd, n_kv), 2 * layer, both, 3,...  252 us
    pallas_call x2, Pallas kernels, body(): call(functools.partial(mlp_kernel, layer, last_layer), 2 * layer + 1, bot...  225 us

profile of v4, /device:TPU:0, one launch (start us, length us, event | category | flops | bytes accessed | tf_op | source)
XLA Modules:
  0.0 479.0 jit_solution(11578983384539787827)
XLA Ops:
  0.0 128.1 %attn0.1 = (f32[256,3072]{1,0:T(8,128)}, bf16[256,3072]{1,0:T(8,128)(2,1)}) custom-call(bf16[256,3072]{1,0:T(8,128)(2,1)} %bitcast.11, bf16[256,3072]{1,0:T(8,128)(2,1)} %bitcast.12, f32[2,3072]{1,0:T(2,128)} %na_ref.7, f32[2,3072]{1,0:T(2,128)} %nm_ref.7, f32[544,128]{1,0:T(8,128)} %constant.2.clone.tab_ref, bf16[2,3,3072,128]{3,2,1,0:T(8,128)(2,1)} %bitcast.7, ...), custom_call_target="tpu_custom_call" | custom-call | tf_op jit(solution)/shard_map/attn0/pallas_call | solution.py:557
  128.1 113.6 %mlp0.1 = (f32[256,3072]{1,0:T(8,128)}, bf16[256,3072]{1,0:T(8,128)(2,1)}) custom-call(f32[256,3072]{1,0:T(8,128)} %get-tuple-element.11.r_h, bf16[256,3072]{1,0:T(8,128)(2,1)} %get-tuple-element.12.a_h, f32[2,3072]{1,0:T(2,128)} %na_ref.7, f32[2,3072]{1,0:T(2,128)} %nm_ref.7, bf16[2,3072,1024]{2,1,0:T(8,128)(2,1)} %wg_h.3, bf16[2,3072,1024]{2,1,0:T(8,128)(2,1)} %wu_h.3, ...), custom_call_target="tpu_custom_call" | custom-call | tf_op jit(solution)/shard_map/mlp0/pallas_call | solution.py:561
  241.8 123.6 %attn1.1 = (f32[256,3072]{1,0:T(8,128)}, bf16[256,3072]{1,0:T(8,128)(2,1)}) custom-call(f32[256,3072]{1,0:T(8,128)} %get-tuple-element.13.r_h, bf16[256,3072]{1,0:T(8,128)(2,1)} %get-tuple-element.14.a_h, f32[2,3072]{1,0:T(2,128)} %na_ref.7, f32[2,3072]{1,0:T(2,128)} %nm_ref.7, f32[544,128]{1,0:T(8,128)} %constant.2.clone.tab_ref, ...), custom_call_target="tpu_custom_call" | custom-call | tf_op jit(solution)/shard_map/attn1/pallas_call | solution.py:557
  365.4 111.0 %mlp1.1 = bf16[256,3072]{1,0:T(8,128)(2,1)} custom-call(f32[256,3072]{1,0:T(8,128)} %get-tuple-element.15.r_h, bf16[256,3072]{1,0:T(8,128)(2,1)} %get-tuple-element.16.a_h, f32[2,3072]{1,0:T(2,128)} %na_ref.7, f32[2,3072]{1,0:T(2,128)} %nm_ref.7, bf16[2,3072,1024]{2,1,0:T(8,128)(2,1)} %wg_h.3, bf16[2,3072,1024]{2,1,0:T(8,128)(2,1)} %wu_h.3, ...), custom_call_target="tpu_custom_call" | custom-call | tf_op jit(solution)/shard_map/mlp1/pallas_call | solution.py:561
  476.4 2.7 copy.12
